TPU v7x, 32 devices: a whole 2x2x4 slice. The times are simulated.
32 devices in a mesh: seq: 8 (over z, y), dp: 4 (over x, core).
Axes of the slice: x: 2, y: 2, z: 4, core: 2. Of those that a mesh axis runs over, the one named last changes fastest.
Arguments:
- attention_queries: bfloat16 [8, 2, 256, 4096], P('seq', None, 'dp'), parts along dimension 2, may hold values from -5.5 to 5.5
- attention_keys: bfloat16 [8, 2, 256, 512], P('seq', None, 'dp'), parts along dimension 2, may hold values from -7.5 to 7.5
- attention_values: bfloat16 [8, 2, 256, 512], P('seq', None, 'dp'), parts along dimension 2, may hold values from -6 to 6
- attention_output: bfloat16 [8, 2, 256, 4096], P('seq', None, 'dp'), parts along dimension 2, may hold values from -6 to 6
- output_gradient: bfloat16 [8, 2, 256, 4096], P('seq', None, 'dp'), parts along dimension 2, may hold values from -48 to 48
- logsumexp_rows: float32 [8, 2, 256, 32], P('seq', None, 'dp'), parts along dimension 2, as said below
Outputs:
- grad_query: float32 [8, 2, 256, 4096], P('seq', None, 'dp'), parts along dimension 2
- key_gradient: float32 [8, 2, 256, 512], P('seq', None, 'dp'), parts along dimension 2
- value_gradient: float32 [8, 2, 256, 512], P('seq', None, 'dp'), parts along dimension 2
There are 4 independent parts, one for each index of `dp`. A program takes and returns all parts, laid end to end along the dimension named above; each array names one. Nothing has to cross between parts.
Inputs may be any that keep to these rules, and one draw needn't show every extreme that they name: logsumexp_rows[i, h] is the logarithm of the sum over key positions t <= i of exp(scores[h, i, t]), computed from attention_queries and attention_keys in float32.
All inputs are finite; a program needn't handle non-finite values.
Results may differ from a plain program's by a relative error of at most 0.0003.
Values may be sent and summed in bfloat16 or wider, within the bound.
A program may use at most 128 MiB of HBM per device.

v0:
```python
import functools

import jax
import jax.numpy as jnp
from jax import lax
from jax.experimental import pallas as pl
from jax.experimental.pallas import tpu as pltpu
from jax.sharding import PartitionSpec as P

HEAD_SIZE = 128
LOG2E = 1.4426950408889634
MESH = pl.DeviceIdType.MESH
KEYS, VALUES = 0, 1
RIGHT, LEFT = 0, 1


def ring_place(index, size):
    return jnp.where(index % 2 == 0, index // 2, size - 1 - index // 2)


def ring_index(place, size):
    return jnp.where(place < size // 2, 2 * place, 2 * (size - 1 - place) + 1)


def split_parts(values):
    high = values.astype(jnp.bfloat16)
    rest = (values - high.astype(jnp.float32)).astype(jnp.bfloat16)
    return jnp.concatenate([high, rest], axis=0)


def dot_rows(a, b):
    return lax.dot_general(a, b, (((1,), (1,)), ((), ())), preferred_element_type=jnp.float32)


def dot(a, b):
    return jnp.dot(a, b, preferred_element_type=jnp.float32)


def kernel(
    n,
    q_ref,
    k_ref,
    v_ref,
    o_ref,
    g_ref,
    lse_ref,
    gq_ref,
    gk_ref,
    gv_ref,
    qs,
    gs,
    delta,
    dqt,
    kv,
    part,
    landed,
    ag_send,
    ag_recv,
    rs_send,
    rs_recv,
):
    half = n // 2
    rows = k_ref.shape[2]
    kv_heads = k_ref.shape[3] // HEAD_SIZE
    group = q_ref.shape[3] // k_ref.shape[3]
    wide = group * rows
    scaling = HEAD_SIZE ** (-0.5)
    me = lax.axis_index("seq")
    place = ring_place(me, n)
    right = ring_index(lax.rem(place + 1, n), n)
    left = ring_index(lax.rem(place + n - 1, n), n)
    target = (right, left)

    barrier = pltpu.get_barrier_semaphore()
    for neighbour in (left, right):
        pl.semaphore_signal(barrier, inc=1, device_id={"seq": neighbour}, device_id_type=MESH)
    pl.semaphore_wait(barrier, 2)

    def gather_copy(way, what, distance, own):
        arrives = n - distance if way == RIGHT else distance
        held = lax.rem(n + 1 - distance, n) if way == RIGHT else distance - 1
        source = (k_ref, v_ref)[what].at[0] if own else kv.at[held, what]
        return pltpu.make_async_remote_copy(
            src_ref=source,
            dst_ref=kv.at[arrives, what],
            send_sem=ag_send.at[way, distance - 1, what],
            recv_sem=ag_recv.at[way, distance - 1, what],
            device_id={"seq": target[way]},
            device_id_type=MESH,
        )

    def sum_copy(what, step, block):
        slot = n - 1 - step if what == KEYS else 1 + step
        return pltpu.make_async_remote_copy(
            src_ref=part.at[what, slot, block],
            dst_ref=landed.at[what, step, block],
            send_sem=rs_send.at[what, step, block],
            recv_sem=rs_recv.at[what, step, block],
            device_id={"seq": target[what]},
            device_id_type=MESH,
        )

    for what in (KEYS, VALUES):
        for way in (RIGHT, LEFT):
            if half > 1 or what == way:
                gather_copy(way, what, 1, True).start()

    def prepare(g, _):
        for a in range(2):
            products = []
            for j in range(group):
                columns = pl.ds(pl.multiple_of((g * group + j) * HEAD_SIZE, HEAD_SIZE), HEAD_SIZE)
                grad = g_ref[0, a, :, columns]
                qs[g, a, pl.ds(j * rows, rows), :] = q_ref[0, a, :, columns]
                gs[g, a, pl.ds(j * rows, rows), :] = grad
                products.append(grad.astype(jnp.float32) * o_ref[0, a, :, columns].astype(jnp.float32))
            turned = jnp.transpose(jnp.concatenate(products, axis=0))
            delta[g, a] = jnp.sum(turned, axis=0, keepdims=True)
            dqt[g, a] = jnp.zeros((HEAD_SIZE, wide), jnp.float32)
        return 0

    lax.fori_loop(0, kv_heads, prepare, 0)

    def unit(key_tile, value_tile, g, a, masked):
        queries, grads = qs[g, a], gs[g, a]
        scores = dot_rows(key_tile, queries)
        weights = jnp.exp2(scores * (scaling * LOG2E) - lse_ref[g, a])
        if masked:
            key_row = lax.broadcasted_iota(jnp.int32, (rows, wide), 0)
            query_row = lax.broadcasted_iota(jnp.int32, (rows, wide), 1) % rows
            weights = jnp.where(key_row <= query_row, weights, 0.0)
        value_part = dot(split_parts(weights), grads)
        score_grad = weights * (dot_rows(value_tile, grads) - delta[g, a])
        split = split_parts(score_grad)
        key_part = dot(split, queries)
        keys_turned = jnp.transpose(jnp.concatenate([key_tile, key_tile], axis=0))
        query_part = dot(keys_turned, split)
        return key_part[:rows] + key_part[rows:], value_part[:rows] + value_part[rows:], query_part

    def columns_of(g):
        return pl.ds(pl.multiple_of(g * HEAD_SIZE, HEAD_SIZE), HEAD_SIZE)

    def shard(slot):
        later = ring_index(lax.rem(place + slot, n), n) > me
        pick = jnp.where(later, 1, 0)

        def head(g, _):
            cols = columns_of(g)
            early = unit(kv[slot, KEYS, 0, :, cols], kv[slot, VALUES, 0, :, cols], g, 1, False)
            other = unit(kv[slot, KEYS, pick, :, cols], kv[slot, VALUES, pick, :, cols], g, pick, False)
            for what in (KEYS, VALUES):
                part[what, slot, 0, :, cols] = early[what] + jnp.where(later, 0.0, other[what])
                part[what, slot, 1, :, cols] = jnp.where(later, other[what], 0.0)
            dqt[g, 1] += early[2]
            dqt[g, pick] += other[2]
            return 0

        lax.fori_loop(0, kv_heads, head, 0)


    def own_shard():
        def head(g, _):
            cols = columns_of(g)
            tiles = [(k_ref[0, b, :, cols], v_ref[0, b, :, cols]) for b in range(2)]
            first = unit(*tiles[0], g, 0, True)
            across = unit(*tiles[0], g, 1, False)
            last = unit(*tiles[1], g, 1, True)
            for what in (KEYS, VALUES):
                part[what, 0, 0, :, cols] = first[what] + across[what]
                part[what, 0, 1, :, cols] = last[what]
            dqt[g, 0] += first[2]
            dqt[g, 1] += across[2] + last[2]
            return 0

        lax.fori_loop(0, kv_heads, head, 0)

    def receive(distance):
        gather_copy(RIGHT, KEYS, distance, False).wait_recv()
        gather_copy(LEFT, VALUES, distance, False).wait_recv()
        gather_copy(RIGHT, VALUES, distance, False).wait_recv()
        gather_copy(LEFT, KEYS, distance, False).wait_recv()

    def send_sums(step, first):
        for block in range(2):
            for what in (KEYS, VALUES):
                if not first:
                    slot = n - 1 - step if what == KEYS else 1 + step
                    sum_copy(what, step - 1, block).wait_recv()
                    part[what, slot, block] += landed[what, step - 1, block]
                sum_copy(what, step, block).start()

    def near(step, first):
        receive(step + 1)

        gather_copy(RIGHT, KEYS, step + 2, False).start()
        gather_copy(LEFT, VALUES, step + 2, False).start()

        @pl.when(step + 2 < half)
        def _():
            gather_copy(RIGHT, VALUES, step + 2, False).start()
            gather_copy(LEFT, KEYS, step + 2, False).start()

        def side(which, _):
            shard(jnp.where(which == 0, n - 1 - step, 1 + step))
            return 0

        lax.fori_loop(0, 2, side, 0)
        send_sums(step, first)

    if half > 1:
        near(0, True)

        def middle(step, _):
            near(step, False)
            return 0

        lax.fori_loop(1, half - 1, middle, 0)

    gather_copy(RIGHT, KEYS, half, False).wait_recv()
    gather_copy(LEFT, VALUES, half, False).wait_recv()
    shard(half)
    send_sums(half - 1, half == 1)

    own_shard()
    for a in range(2):
        def write(g, _):
            turned = jnp.transpose(dqt[g, a]) * scaling
            for j in range(group):
                columns = pl.ds(pl.multiple_of((g * group + j) * HEAD_SIZE, HEAD_SIZE), HEAD_SIZE)
                gq_ref[0, a, :, columns] = turned[j * rows : (j + 1) * rows]
            return 0

        lax.fori_loop(0, kv_heads, write, 0)

    def far(step, _):
        send_sums(step, False)
        return 0

    lax.fori_loop(half, n - 1, far, 0)
    for block in range(2):
        for what in (KEYS, VALUES):
            sum_copy(what, n - 2, block).wait_recv()
            total = part[what, 0, block] + landed[what, n - 2, block]
            if what == KEYS:
                gk_ref[0, block] = total * scaling
            else:
                gv_ref[0, block] = total

    def sent(step, _):
        for block in range(2):
            for what in (KEYS, VALUES):
                sum_copy(what, step, block).wait_send()
        return 0

    lax.fori_loop(0, n - 1, sent, 0)

    def passed(distance, _):
        gather_copy(RIGHT, KEYS, distance, False).wait_send()
        gather_copy(LEFT, VALUES, distance, False).wait_send()
        gather_copy(RIGHT, VALUES, distance, False).wait_send()
        gather_copy(LEFT, KEYS, distance, False).wait_send()
        return 0

    lax.fori_loop(1, half, passed, 0)
    gather_copy(RIGHT, KEYS, half, False).wait_send()
    gather_copy(LEFT, VALUES, half, False).wait_send()


def body(queries, keys, values, output, gradient, logsumexp):
    n = lax.axis_size("seq")
    rows = keys.shape[2]
    kv_heads = keys.shape[3] // HEAD_SIZE
    group = queries.shape[3] // keys.shape[3]
    wide = group * rows
    lse = logsumexp[0].reshape(2, rows, kv_heads, group).transpose(2, 0, 3, 1)
    lse = (lse * LOG2E).reshape(kv_heads, 2, 1, wide)
    vmem = pl.BlockSpec(memory_space=pltpu.VMEM)
    pair = (2, rows, keys.shape[3])
    return pl.pallas_call(
        functools.partial(kernel, n),
        out_shape=(
            jax.ShapeDtypeStruct(queries.shape, jnp.float32),
            jax.ShapeDtypeStruct(keys.shape, jnp.float32),
            jax.ShapeDtypeStruct(values.shape, jnp.float32),
        ),
        in_specs=[vmem] * 6,
        out_specs=(vmem, vmem, vmem),
        scratch_shapes=[
            pltpu.VMEM((kv_heads, 2, wide, HEAD_SIZE), jnp.bfloat16),
            pltpu.VMEM((kv_heads, 2, wide, HEAD_SIZE), jnp.bfloat16),
            pltpu.VMEM((kv_heads, 2, 1, wide), jnp.float32),
            pltpu.VMEM((kv_heads, 2, HEAD_SIZE, wide), jnp.float32),
            pltpu.VMEM((n, 2) + pair, jnp.bfloat16),
            pltpu.VMEM((2, n) + pair, jnp.float32),
            pltpu.VMEM((2, n - 1) + pair, jnp.float32),
            pltpu.SemaphoreType.DMA((2, n // 2, 2)),
            pltpu.SemaphoreType.DMA((2, n // 2, 2)),
            pltpu.SemaphoreType.DMA((2, n - 1, 2)),
            pltpu.SemaphoreType.DMA((2, n - 1, 2)),
        ],
        compiler_params=pltpu.CompilerParams(
            collective_id=0, has_side_effects=True, vmem_limit_bytes=64_000_000
        ),
    )(queries, keys, values, output, gradient, lse)


def solution(mesh):
    spec = P("seq", None, "dp", None)
    return jax.shard_map(
        body, mesh=mesh, in_specs=(spec,) * 6, out_specs=(spec,) * 3, check_vma=False
    )
```

profile of v0, /device:TPU:0, one launch (start us, length us, event | category | flops | bytes accessed | tf_op | source)
XLA Modules:
  0.0 81.1 jit_solution(6668678417634184534)
XLA Ops:
  0.6 0.8 copy_bitcast_fusion
  1.4 0.7 reshape.11.lse_ref
  2.1 74.4 %shard_map.85 = (f32[1,2,64,4096]{3,2,1,0:T(8,128)}, f32[1,2,64,512]{3,2,1,0:T(8,128)}, f32[1,2,64,512]{3,2,1,0:T(8,128)}) custom-call(bf16[1,2,64,4096]{3,2,1,0:T(8,128)(2,1)} %q_ref.1, bf16[1,2,64,512]{3,2,1,0:T(8,128)(2,1)} %k_ref.1, bf16[1,2,64,512]{3,2,1,0:T(8,128)(2,1)} %v_ref.1, bf16[1,2,64,4096]{3,2,1,0:T(8,128)(2,1)} %o_ref.1, ...), custom_call_target="tpu_custom_call" | custom-call | tf_op jit(solution)/shard_map/pallas_call | solution.py:279
  76.5 0.0 copy-start.1
  76.5 0.0 copy-start
  76.5 3.2 %copy.14 = f32[1,2,64,4096]{3,2,1,0:T(8,128)} copy(f32[1,2,64,4096]{3,2,1,0:T(8,128)} %get-tuple-element.6) | data formatting | bytes 4194304
  79.7 0.0 copy-done.1
  79.7 0.7 copy.15
  80.4 0.0 copy-done
  80.4 0.7 copy.16
Async XLA Ops:
  76.5 3.2 %copy-start.1 = (f32[1,2,64,512]{3,2,1,0:T(8,128)S(1)}, f32[1,2,64,512]{3,2,1,0:T(8,128)}, u32[]{:S(2)}) copy-start(f32[1,2,64,512]{3,2,1,0:T(8,128)} %get-tuple-element.7) | copy-start | bytes 786436
  76.5 3.9 %copy-start = (f32[1,2,64,512]{3,2,1,0:T(8,128)S(1)}, f32[1,2,64,512]{3,2,1,0:T(8,128)}, u32[]{:S(2)}) copy-start(f32[1,2,64,512]{3,2,1,0:T(8,128)} %get-tuple-element.8) | copy-start | bytes 786436
where the time goes:
time: 81.3 us; the launch traced here: 81.1 us
  Pallas kernels  74.4 us (92%)
  local copies, waits for them, and re-layouts  5.27 us (6%)
    pallas_call x1, Pallas kernels, body(): pl.pallas_call(functools.partial(kernel, n), out_shape=(jax.ShapeDtypeStr...  74.4 us
    unnamed x7, local copies, waits for them, and re-layouts  4.58 us

commit v1 on v0

v1 whole, which is shorter than its diff:
```python
import functools

import jax
import jax.numpy as jnp
from jax import lax
from jax.experimental import pallas as pl
from jax.experimental.pallas import tpu as pltpu
from jax.sharding import PartitionSpec as P

HEAD_SIZE = 128
LOG2E = 1.4426950408889634
LN2 = 0.6931471805599453
SPAN = 240.0
MESH = pl.DeviceIdType.MESH
KEYS, VALUES = 0, 1
RIGHT, LEFT = 0, 1


def ring_place(index, size):
    return jnp.where(index % 2 == 0, index // 2, size - 1 - index // 2)


def ring_index(place, size):
    return jnp.where(place < size // 2, 2 * place, 2 * (size - 1 - place) + 1)


def split_parts(values):
    high = values.astype(jnp.bfloat16)
    rest = (values - high.astype(jnp.float32)).astype(jnp.bfloat16)
    return jnp.concatenate([high, rest], axis=0)


def dot(a, b):
    return jnp.dot(a, b, preferred_element_type=jnp.float32)


def encode(values):
    scale = jnp.maximum(jnp.max(jnp.abs(values), axis=0, keepdims=True), 1e-30)
    level = values * (SPAN / scale)
    code = jnp.exp2(jnp.abs(level) - 0.5 * SPAN)
    return jnp.where(level < 0.0, -code, code).astype(jnp.bfloat16), scale


def decode(code, scale):
    code = code.astype(jnp.float32)
    size = jnp.log(jnp.abs(code)) * (scale * (1.0 / (SPAN * LN2))) + 0.5 * scale
    return jnp.where(code < 0.0, -size, size)


def kernel(
    n,
    q_ref,
    k_ref,
    v_ref,
    o_ref,
    g_ref,
    lse_ref,
    gq_ref,
    gk_ref,
    gv_ref,
    qs,
    gs,
    qt,
    gt,
    delta,
    dqt,
    kv,
    part,
    coded,
    scales,
    landed,
    landed_scales,
    ag_send,
    ag_recv,
    rs_send,
    rs_recv,
):
    half = n // 2
    rows = k_ref.shape[2]
    kv_heads = k_ref.shape[3] // HEAD_SIZE
    group = q_ref.shape[3] // k_ref.shape[3]
    wide = group * rows
    scaling = HEAD_SIZE ** (-0.5)
    me = lax.axis_index("seq")
    place = ring_place(me, n)
    right = ring_index(lax.rem(place + 1, n), n)
    left = ring_index(lax.rem(place + n - 1, n), n)
    target = (right, left)

    barrier = pltpu.get_barrier_semaphore()
    for neighbour in (left, right):
        pl.semaphore_signal(barrier, inc=1, device_id={"seq": neighbour}, device_id_type=MESH)
    pl.semaphore_wait(barrier, 2)

    def gather_copy(way, what, distance, own):
        arrives = n - distance if way == RIGHT else distance
        held = lax.rem(n + 1 - distance, n) if way == RIGHT else distance - 1
        source = (k_ref, v_ref)[what].at[0] if own else kv.at[held, what]
        return pltpu.make_async_remote_copy(
            src_ref=source,
            dst_ref=kv.at[arrives, what],
            send_sem=ag_send.at[way, distance - 1, what],
            recv_sem=ag_recv.at[way, distance - 1, what],
            device_id={"seq": target[way]},
            device_id_type=MESH,
        )

    def sum_copies(what, step, block):
        return [
            pltpu.make_async_remote_copy(
                src_ref=source.at[what, step, block],
                dst_ref=sink.at[what, step, block],
                send_sem=rs_send.at[what, step, block, i],
                recv_sem=rs_recv.at[what, step, block, i],
                device_id={"seq": target[what]},
                device_id_type=MESH,
            )
            for i, (source, sink) in enumerate(((coded, landed), (scales, landed_scales)))
        ]

    for what in (KEYS, VALUES):
        for way in (RIGHT, LEFT):
            if half > 1 or what == way:
                gather_copy(way, what, 1, True).start()

    def prepare(g, _):
        for a in range(2):
            products = []
            for j in range(group):
                columns = pl.ds(pl.multiple_of((g * group + j) * HEAD_SIZE, HEAD_SIZE), HEAD_SIZE)
                grad = g_ref[0, a, :, columns]
                qs[g, a, pl.ds(j * rows, rows), :] = q_ref[0, a, :, columns]
                gs[g, a, pl.ds(j * rows, rows), :] = grad
                products.append(grad.astype(jnp.float32) * o_ref[0, a, :, columns].astype(jnp.float32))
            turned = jnp.transpose(jnp.concatenate(products, axis=0))
            delta[g, a] = jnp.sum(turned, axis=0, keepdims=True)
            qt[g, a] = jnp.transpose(qs[g, a])
            gt[g, a] = jnp.transpose(gs[g, a])
        return 0

    lax.fori_loop(0, kv_heads, prepare, 0)

    def unit(keys, values, g, a, mask=None):
        count = keys.shape[0]
        scores = dot(keys, qt[g, a])
        weights = jnp.exp2(scores * (scaling * LOG2E) - lse_ref[g, a])
        if mask is not None:
            weights = jnp.where(mask, weights, 0.0)
        value_part = dot(split_parts(weights), gs[g, a])
        score_grad = weights * (dot(values, gt[g, a]) - delta[g, a])
        split = split_parts(score_grad)
        key_part = dot(split, qs[g, a])
        turned = jnp.transpose(keys)
        query_part = dot(jnp.concatenate([turned, turned], axis=1), split)
        return key_part[:count] + key_part[count:], value_part[:count] + value_part[count:], query_part

    def columns_of(g):
        return pl.ds(pl.multiple_of(g * HEAD_SIZE, HEAD_SIZE), HEAD_SIZE)

    def for_heads(head):
        def one(g, _):
            head(g, columns_of(g))
            return 0

        lax.fori_loop(0, kv_heads, one, 0, unroll=UNROLL)

    def shard(slot):
        later = ring_index(lax.rem(place + slot, n), n) > me

        @pl.when(later)
        def _():
            def head(g, cols):
                keys = kv[slot, KEYS, :, :, cols].reshape(2 * rows, HEAD_SIZE)
                values = kv[slot, VALUES, :, :, cols].reshape(2 * rows, HEAD_SIZE)
                out = unit(keys, values, g, 1)
                for what in (KEYS, VALUES):
                    part[what, slot, :, :, cols] = out[what].reshape(2, rows, HEAD_SIZE)
                dqt[g, 1] += out[2]

            for_heads(head)

        @pl.when(jnp.logical_not(later))
        def _():
            def head(g, cols):
                keys = kv[slot, KEYS, 0, :, cols]
                values = kv[slot, VALUES, 0, :, cols]
                outs = [unit(keys, values, g, a) for a in range(2)]
                for what in (KEYS, VALUES):
                    part[what, slot, 0, :, cols] = outs[0][what] + outs[1][what]
                    part[what, slot, 1, :, cols] = jnp.zeros((rows, HEAD_SIZE), jnp.float32)
                for a in range(2):
                    dqt[g, a] += outs[a][2]

            for_heads(head)

    def own_shard():
        def head(g, cols):
            key_row = lax.broadcasted_iota(jnp.int32, (2 * rows, wide), 0)
            query_row = lax.broadcasted_iota(jnp.int32, (2 * rows, wide), 1) % rows
            keys = k_ref[0, :, :, cols].reshape(2 * rows, HEAD_SIZE)
            values = v_ref[0, :, :, cols].reshape(2 * rows, HEAD_SIZE)
            first = unit(keys[:rows], values[:rows], g, 0, key_row[:rows] <= query_row[:rows])
            second = unit(keys, values, g, 1, key_row <= query_row + rows)
            for what in (KEYS, VALUES):
                part[what, 0, 0, :, cols] = first[what] + second[what][:rows]
                part[what, 0, 1, :, cols] = second[what][rows:]
            dqt[g, 0] = first[2]
            dqt[g, 1] = second[2]

        for_heads(head)

    own_shard()

    def send_sums(step, first):
        for block in range(2):
            for what in (KEYS, VALUES):
                slot = n - 1 - step if what == KEYS else 1 + step
                total = part[what, slot, block]
                if not first:
                    for copy in sum_copies(what, step - 1, block):
                        copy.wait_recv()
                    total += decode(landed[what, step - 1, block], landed_scales[what, step - 1, block])
                coded[what, step, block], scales[what, step, block] = encode(total)
                for copy in sum_copies(what, step, block):
                    copy.start()

    def near(step, first):
        gather_copy(RIGHT, KEYS, step + 1, False).wait_recv()
        gather_copy(RIGHT, KEYS, step + 2, False).start()
        gather_copy(LEFT, VALUES, step + 1, False).wait_recv()
        gather_copy(LEFT, VALUES, step + 2, False).start()
        for way, what in ((RIGHT, VALUES), (LEFT, KEYS)):
            gather_copy(way, what, step + 1, False).wait_recv()

            @pl.when(step + 2 < half)
            def _():
                gather_copy(way, what, step + 2, False).start()

        def side(which, _):
            shard(jnp.where(which == 0, n - 1 - step, 1 + step))
            return 0

        lax.fori_loop(0, 2, side, 0)
        send_sums(step, first)

    if half > 1:
        near(0, True)

        def middle(step, _):
            near(step, False)
            return 0

        lax.fori_loop(1, half - 1, middle, 0)

    gather_copy(RIGHT, KEYS, half, False).wait_recv()
    gather_copy(LEFT, VALUES, half, False).wait_recv()
    shard(half)
    send_sums(half - 1, half == 1)

    for a in range(2):

        def write(g, _):
            turned = jnp.transpose(dqt[g, a]) * scaling
            for j in range(group):
                columns = pl.ds(pl.multiple_of((g * group + j) * HEAD_SIZE, HEAD_SIZE), HEAD_SIZE)
                gq_ref[0, a, :, columns] = turned[j * rows : (j + 1) * rows]
            return 0

        lax.fori_loop(0, kv_heads, write, 0)

    def far(step, _):
        send_sums(step, False)
        return 0

    lax.fori_loop(half, n - 1, far, 0)
    for block in range(2):
        for what in (KEYS, VALUES):
            for copy in sum_copies(what, n - 2, block):
                copy.wait_recv()
            total = part[what, 0, block] + decode(landed[what, n - 2, block], landed_scales[what, n - 2, block])
            if what == KEYS:
                gk_ref[0, block] = total * scaling
            else:
                gv_ref[0, block] = total

    def sent(step, _):
        for block in range(2):
            for what in (KEYS, VALUES):
                for copy in sum_copies(what, step, block):
                    copy.wait_send()
        return 0

    lax.fori_loop(0, n - 1, sent, 0)

    def passed(distance, _):
        gather_copy(RIGHT, KEYS, distance, False).wait_send()
        gather_copy(LEFT, VALUES, distance, False).wait_send()
        gather_copy(RIGHT, VALUES, distance, False).wait_send()
        gather_copy(LEFT, KEYS, distance, False).wait_send()
        return 0

    lax.fori_loop(1, half, passed, 0)
    gather_copy(RIGHT, KEYS, half, False).wait_send()
    gather_copy(LEFT, VALUES, half, False).wait_send()


UNROLL = True


def body(queries, keys, values, output, gradient, logsumexp):
    n = lax.axis_size("seq")
    rows = keys.shape[2]
    kv_heads = keys.shape[3] // HEAD_SIZE
    group = queries.shape[3] // keys.shape[3]
    wide = group * rows
    lse = logsumexp[0].reshape(2, rows, kv_heads, group).transpose(2, 0, 3, 1)
    lse = (lse * LOG2E).reshape(kv_heads, 2, 1, wide)
    vmem = pl.BlockSpec(memory_space=pltpu.VMEM)
    pair = (2, rows, keys.shape[3])
    scale = (2, 1, keys.shape[3])
    return pl.pallas_call(
        functools.partial(kernel, n),
        out_shape=(
            jax.ShapeDtypeStruct(queries.shape, jnp.float32),
            jax.ShapeDtypeStruct(keys.shape, jnp.float32),
            jax.ShapeDtypeStruct(values.shape, jnp.float32),
        ),
        in_specs=[vmem] * 6,
        out_specs=(vmem, vmem, vmem),
        scratch_shapes=[
            pltpu.VMEM((kv_heads, 2, wide, HEAD_SIZE), jnp.bfloat16),
            pltpu.VMEM((kv_heads, 2, wide, HEAD_SIZE), jnp.bfloat16),
            pltpu.VMEM((kv_heads, 2, HEAD_SIZE, wide), jnp.bfloat16),
            pltpu.VMEM((kv_heads, 2, HEAD_SIZE, wide), jnp.bfloat16),
            pltpu.VMEM((kv_heads, 2, 1, wide), jnp.float32),
            pltpu.VMEM((kv_heads, 2, HEAD_SIZE, wide), jnp.float32),
            pltpu.VMEM((n, 2) + pair, jnp.bfloat16),
            pltpu.VMEM((2, n) + pair, jnp.float32),
            pltpu.VMEM((2, n - 1) + pair, jnp.bfloat16),
            pltpu.VMEM((2, n - 1) + scale, jnp.float32),
            pltpu.VMEM((2, n - 1) + pair, jnp.bfloat16),
            pltpu.VMEM((2, n - 1) + scale, jnp.float32),
            pltpu.SemaphoreType.DMA((2, n // 2, 2)),
            pltpu.SemaphoreType.DMA((2, n // 2, 2)),
            pltpu.SemaphoreType.DMA((2, n - 1, 2, 2)),
            pltpu.SemaphoreType.DMA((2, n - 1, 2, 2)),
        ],
        compiler_params=pltpu.CompilerParams(
            collective_id=0, has_side_effects=True, vmem_limit_bytes=64_000_000
        ),
    )(queries, keys, values, output, gradient, lse)


def solution(mesh):
    spec = P("seq", None, "dp", None)
    return jax.shard_map(
        body, mesh=mesh, in_specs=(spec,) * 6, out_specs=(spec,) * 3, check_vma=False
    )
```

time: 81.3 us -> 68.3 us (0.84)
  Pallas kernels: 74.4 us -> 61.4 us
    pallas_call x1, Pallas kernels: 74.4 us -> 61.4 us  [body(): pl.pallas_call(functools.partial(kernel, n), out_shape=(jax.ShapeDtypeStr...]
where the time goes in v1:
time: 68.3 us; the launch traced here: 68.1 us
  Pallas kernels  61.4 us (90%)
  local copies, waits for them, and re-layouts  5.27 us (8%)
  other arithmetic  0.76 us (1%)
    pallas_call x1, Pallas kernels, body(): pl.pallas_call(functools.partial(kernel, n), out_shape=(jax.ShapeDtypeStr...  61.4 us
    unnamed x7, local copies, waits for them, and re-layouts  4.58 us

profile of v1, /device:TPU:0, one launch (start us, length us, event | category | flops | bytes accessed | tf_op | source)
XLA Modules:
  0.0 68.1 jit_solution(10706351384759444059)
XLA Ops:
  0.6 0.8 %copy_bitcast_fusion = f32[4,2,8,64]{3,2,1,0:T(8,128)S(1)} fusion(f32[1,2,64,32]{2,3,1,0:T(8,128)} %param.11), kind=kLoop, calls=%fused_computation | loop fusion | flops 4096 | bytes 32768 | tf_op jit(solution)/shard_map/mul | solution.py:317
  1.4 0.7 %reshape.11.lse_ref = f32[4,2,1,512]{3,2,1,0:T(1,128)} reshape(f32[4,2,8,64]{3,2,1,0:T(8,128)S(1)} %copy_bitcast_fusion) | data formatting | bytes 32768 | tf_op jit(solution)/shard_map/reshape | solution.py:317
  2.1 61.4 %shard_map.85 = (f32[1,2,64,4096]{3,2,1,0:T(8,128)}, f32[1,2,64,512]{3,2,1,0:T(8,128)}, f32[1,2,64,512]{3,2,1,0:T(8,128)}) custom-call(bf16[1,2,64,4096]{3,2,1,0:T(8,128)(2,1)} %q_ref.1, bf16[1,2,64,512]{3,2,1,0:T(8,128)(2,1)} %k_ref.1, bf16[1,2,64,512]{3,2,1,0:T(8,128)(2,1)} %v_ref.1, bf16[1,2,64,4096]{3,2,1,0:T(8,128)(2,1)} %o_ref.1, ...), custom_call_target="tpu_custom_call" | custom-call | tf_op jit(solution)/shard_map/pallas_call | solution.py:321
  63.5 0.0 copy-start.1
  63.5 0.0 copy-start
  63.5 3.2 %copy.14 = f32[1,2,64,4096]{3,2,1,0:T(8,128)} copy(f32[1,2,64,4096]{3,2,1,0:T(8,128)} %get-tuple-element.6) | data formatting | bytes 4194304
  66.7 0.0 copy-done.1
  66.7 0.7 %copy.15 = f32[1,2,64,512]{3,2,1,0:T(8,128)} copy(f32[1,2,64,512]{3,2,1,0:T(8,128)S(1)} %copy-done.1) | data formatting | bytes 524288
  67.4 0.0 copy-done
  67.4 0.7 %copy.16 = f32[1,2,64,512]{3,2,1,0:T(8,128)} copy(f32[1,2,64,512]{3,2,1,0:T(8,128)S(1)} %copy-done) | data formatting | bytes 524288
Async XLA Ops:
  63.5 3.2 %copy-start.1 = (f32[1,2,64,512]{3,2,1,0:T(8,128)S(1)}, f32[1,2,64,512]{3,2,1,0:T(8,128)}, u32[]{:S(2)}) copy-start(f32[1,2,64,512]{3,2,1,0:T(8,128)} %get-tuple-element.7) | copy-start | bytes 786436
  63.5 3.9 %copy-start = (f32[1,2,64,512]{3,2,1,0:T(8,128)S(1)}, f32[1,2,64,512]{3,2,1,0:T(8,128)}, u32[]{:S(2)}) copy-start(f32[1,2,64,512]{3,2,1,0:T(8,128)} %get-tuple-element.8) | copy-start | bytes 786436

commit v2 on v1

v2 whole, which is shorter than its diff:
```python
import functools

import jax
import jax.numpy as jnp
from jax import lax
from jax.experimental import pallas as pl
from jax.experimental.pallas import tpu as pltpu
from jax.sharding import PartitionSpec as P

HEAD_SIZE = 128
LOG2E = 1.4426950408889634
LN2 = 0.6931471805599453
SPAN = 240.0
MESH = pl.DeviceIdType.MESH
KEYS, VALUES = 0, 1
HALVES = 2
RIGHT, LEFT = 0, 1


def ring_place(index, size):
    return jnp.where(index % 2 == 0, index // 2, size - 1 - index // 2)


def ring_index(place, size):
    return jnp.where(place < size // 2, 2 * place, 2 * (size - 1 - place) + 1)


def split_parts(values):
    high = values.astype(jnp.bfloat16)
    rest = (values - high.astype(jnp.float32)).astype(jnp.bfloat16)
    return jnp.concatenate([high, rest], axis=0)


def dot(a, b):
    return jnp.dot(a, b, preferred_element_type=jnp.float32)


def encode(values):
    scale = jnp.maximum(jnp.max(jnp.abs(values), axis=0, keepdims=True), 1e-30)
    level = values * (SPAN / scale)
    code = jnp.exp2(jnp.abs(level) - 0.5 * SPAN)
    return jnp.where(level < 0.0, -code, code).astype(jnp.bfloat16), scale


def decode(code, scale):
    code = code.astype(jnp.float32)
    size = jnp.log(jnp.abs(code)) * (scale * (1.0 / (SPAN * LN2))) + 0.5 * scale
    return jnp.where(code < 0.0, -size, size)


def kernel(
    n,
    q_hbm,
    k_hbm,
    v_hbm,
    o_hbm,
    g_hbm,
    lse_hbm,
    dqt,
    gk_ref,
    gv_ref,
    q_ref,
    o_ref,
    g_ref,
    lse_ref,
    qs,
    gs,
    qt,
    gt,
    delta,
    lse,
    kv,
    part,
    coded,
    scales,
    landed,
    landed_scales,
    load_sem,
    own_sem,
    ag_send,
    ag_recv,
    rs_send,
    rs_recv,
):
    half = n // 2
    rows = k_hbm.shape[2]
    kv_heads = k_hbm.shape[3] // HEAD_SIZE
    some = kv_heads // HALVES
    columns = some * HEAD_SIZE
    group = q_hbm.shape[3] // k_hbm.shape[3]
    wide = group * rows
    scaling = HEAD_SIZE ** (-0.5)
    me = lax.axis_index("seq")
    place = ring_place(me, n)
    right = ring_index(lax.rem(place + 1, n), n)
    left = ring_index(lax.rem(place + n - 1, n), n)
    target = (right, left)

    own = [
        pltpu.make_async_copy(
            source.at[0, :, :, pl.ds(h * columns, columns)], kv.at[0, h, what], own_sem.at[h, what]
        )
        for h in range(HALVES)
        for what, source in ((KEYS, k_hbm), (VALUES, v_hbm))
    ]
    loads = [
        pltpu.make_async_copy(source, sink, load_sem.at[i])
        for i, (source, sink) in enumerate(
            ((q_hbm, q_ref), (g_hbm, g_ref), (o_hbm, o_ref), (lse_hbm, lse_ref))
        )
    ]
    for copy in own + loads:
        copy.start()

    barrier = pltpu.get_barrier_semaphore()
    for neighbour in (left, right):
        pl.semaphore_signal(barrier, inc=1, device_id={"seq": neighbour}, device_id_type=MESH)
    pl.semaphore_wait(barrier, 2)

    def gather_copy(way, h, distance):
        arrives = n - distance if way == RIGHT else distance
        held = lax.rem(n + 1 - distance, n) if way == RIGHT else distance - 1
        return pltpu.make_async_remote_copy(
            src_ref=kv.at[held, h],
            dst_ref=kv.at[arrives, h],
            send_sem=ag_send.at[way, distance - 1, h],
            recv_sem=ag_recv.at[way, distance - 1, h],
            device_id={"seq": target[way]},
            device_id_type=MESH,
        )

    def sum_copies(way, step, what):
        return [
            pltpu.make_async_remote_copy(
                src_ref=source.at[way, step, what],
                dst_ref=sink.at[way, step, what],
                send_sem=rs_send.at[way, step, what, i],
                recv_sem=rs_recv.at[way, step, what, i],
                device_id={"seq": target[way]},
                device_id_type=MESH,
            )
            for i, (source, sink) in enumerate(((coded, landed), (scales, landed_scales)))
        ]

    for copy in own:
        copy.wait()
    for turn in range(HALVES):
        for way in (RIGHT, LEFT):
            if half > 1 or turn == 0:
                gather_copy(way, way if turn == 0 else 1 - way, 1).start()
    for copy in loads:
        copy.wait()

    def prepare(g, _):
        for a in range(2):
            products = []
            for j in range(group):
                head = pl.ds(pl.multiple_of((g * group + j) * HEAD_SIZE, HEAD_SIZE), HEAD_SIZE)
                grad = g_ref[0, a, :, head]
                qs[g, a, pl.ds(j * rows, rows), :] = q_ref[0, a, :, head]
                gs[g, a, pl.ds(j * rows, rows), :] = grad
                products.append(grad.astype(jnp.float32) * o_ref[0, a, :, head].astype(jnp.float32))
            turned = jnp.transpose(jnp.concatenate(products, axis=0))
            delta[g, a] = jnp.sum(turned, axis=0, keepdims=True)
            qt[g, a] = jnp.transpose(qs[g, a])
            gt[g, a] = jnp.transpose(gs[g, a])
            tile = lse_ref[0, a, pl.ds(pl.multiple_of(g * group, group), group), :] * LOG2E
            lse[g, a] = jnp.concatenate([tile[j : j + 1] for j in range(group)], axis=1)
        return 0

    lax.fori_loop(0, kv_heads, prepare, 0)

    def unit(keys, values, g, a, mask=None):
        count = keys.shape[0]
        scores = dot(keys, qt[g, a])
        weights = jnp.exp2(scores * (scaling * LOG2E) - lse[g, a])
        if mask is not None:
            weights = jnp.where(mask, weights, 0.0)
        value_part = dot(split_parts(weights), gs[g, a])
        score_grad = weights * (dot(values, gt[g, a]) - delta[g, a])
        split = split_parts(score_grad)
        key_part = dot(split, qs[g, a])
        turned = jnp.transpose(keys)
        query_part = dot(jnp.concatenate([turned, turned], axis=1), split)
        return key_part[:count] + key_part[count:], value_part[:count] + value_part[count:], query_part

    def later_shard(slot, h, i):
        cols = pl.ds(i * HEAD_SIZE, HEAD_SIZE)
        g = h * some + i
        keys = kv[slot, h, KEYS, :, :, cols].reshape(2 * rows, HEAD_SIZE)
        values = kv[slot, h, VALUES, :, :, cols].reshape(2 * rows, HEAD_SIZE)
        out = unit(keys, values, g, 1)
        for what in (KEYS, VALUES):
            part[slot, h, what, :, :, cols] = out[what].reshape(2, rows, HEAD_SIZE)
        dqt[g, 1] += out[2]

    def earlier_shard(slot, h, i):
        cols = pl.ds(i * HEAD_SIZE, HEAD_SIZE)
        g = h * some + i
        keys = kv[slot, h, KEYS, 0, :, cols]
        values = kv[slot, h, VALUES, 0, :, cols]
        outs = [unit(keys, values, g, a) for a in range(2)]
        for what in (KEYS, VALUES):
            part[slot, h, what, 0, :, cols] = outs[0][what] + outs[1][what]
            part[slot, h, what, 1, :, cols] = jnp.zeros((rows, HEAD_SIZE), jnp.float32)
        for a in range(2):
            dqt[g, a] += outs[a][2]

    def shard(slot, h):
        later = ring_index(lax.rem(place + slot, n), n) > me

        @pl.when(later)
        def _():
            for i in range(some):
                later_shard(slot, h, i)

        @pl.when(jnp.logical_not(later))
        def _():
            for i in range(some):
                earlier_shard(slot, h, i)

    def own_shard(h, i):
        cols = pl.ds(i * HEAD_SIZE, HEAD_SIZE)
        g = h * some + i
        key_row = lax.broadcasted_iota(jnp.int32, (2 * rows, wide), 0)
        query_row = lax.broadcasted_iota(jnp.int32, (2 * rows, wide), 1) % rows
        keys = kv[0, h, KEYS, :, :, cols].reshape(2 * rows, HEAD_SIZE)
        values = kv[0, h, VALUES, :, :, cols].reshape(2 * rows, HEAD_SIZE)
        first = unit(keys[:rows], values[:rows], g, 0, key_row[:rows] <= query_row[:rows])
        second = unit(keys, values, g, 1, key_row <= query_row + rows)
        for what in (KEYS, VALUES):
            part[0, h, what, 0, :, cols] = first[what] + second[what][:rows]
            part[0, h, what, 1, :, cols] = second[what][rows:]
        dqt[g, 0] = first[2]
        dqt[g, 1] = second[2]

    def own_half(h, _):
        for i in range(some):
            own_shard(h, i)
        return 0

    lax.fori_loop(0, HALVES, own_half, 0)

    def slot_of(way, step):
        return n - 1 - step if way == RIGHT else 1 + step

    def send_sums(way, step, first):
        for what in (KEYS, VALUES):
            if not first:
                for copy in sum_copies(way, step - 1, what):
                    copy.wait_recv()
            for block in range(2):
                total = part[slot_of(way, step), way, what, block]
                if not first:
                    total += decode(landed[way, step - 1, what, block], landed_scales[way, step - 1, what, block])
                coded[way, step, what, block], scales[way, step, what, block] = encode(total)
            for copy in sum_copies(way, step, what):
                copy.start()

    def near(step, first):
        for way in (RIGHT, LEFT):
            gather_copy(way, way, step + 1).wait_recv()
            gather_copy(way, way, step + 2).start()
        for way in (RIGHT, LEFT):
            shard(slot_of(way, step), way)
            send_sums(way, step, first)
        for way in (RIGHT, LEFT):
            gather_copy(way, 1 - way, step + 1).wait_recv()

            @pl.when(step + 2 < half)
            def _():
                gather_copy(way, 1 - way, step + 2).start()

        for way in (RIGHT, LEFT):
            shard(slot_of(way, step), 1 - way)

    if half > 1:
        near(0, True)

        def middle(step, _):
            near(step, False)
            return 0

        lax.fori_loop(1, half - 1, middle, 0)

    for way in (RIGHT, LEFT):
        gather_copy(way, way, half).wait_recv()
        shard(half, way)
        send_sums(way, half - 1, half == 1)

    def far(step, _):
        for way in (RIGHT, LEFT):
            send_sums(way, step, False)
        return 0

    lax.fori_loop(half, n - 1, far, 0)
    for way in (RIGHT, LEFT):
        cols = pl.ds(way * columns, columns)
        for what in (KEYS, VALUES):
            for copy in sum_copies(way, n - 2, what):
                copy.wait_recv()
            for block in range(2):
                total = part[0, way, what, block]
                total += decode(landed[way, n - 2, what, block], landed_scales[way, n - 2, what, block])
                if what == KEYS:
                    gk_ref[0, block, :, cols] = total * scaling
                else:
                    gv_ref[0, block, :, cols] = total

    def sent(step, _):
        for way in (RIGHT, LEFT):
            for what in (KEYS, VALUES):
                for copy in sum_copies(way, step, what):
                    copy.wait_send()
        return 0

    lax.fori_loop(0, n - 1, sent, 0)

    def passed(distance, _):
        for way in (RIGHT, LEFT):
            for h in range(HALVES):
                gather_copy(way, h, distance).wait_send()
        return 0

    lax.fori_loop(1, half, passed, 0)
    for way in (RIGHT, LEFT):
        gather_copy(way, way, half).wait_send()


def finish(dqt, gk_in, gv_in, gq_ref, gk_ref, gv_ref):
    kv_heads, _, _, wide = dqt.shape
    rows = gq_ref.shape[2]
    for g in range(kv_heads):
        for a in range(2):
            turned = jnp.transpose(dqt[g, a]) * HEAD_SIZE ** (-0.5)
            for j in range(wide // rows):
                head = pl.ds((g * (wide // rows) + j) * HEAD_SIZE, HEAD_SIZE)
                gq_ref[0, a, :, head] = turned[j * rows : (j + 1) * rows]
    gk_ref[...] = gk_in[...]
    gv_ref[...] = gv_in[...]


def body(queries, keys, values, output, gradient, logsumexp):
    n = lax.axis_size("seq")
    rows = keys.shape[2]
    kv_heads = keys.shape[3] // HEAD_SIZE
    group = queries.shape[3] // keys.shape[3]
    wide = group * rows
    lse = logsumexp.transpose(0, 1, 3, 2)
    vmem = pl.BlockSpec(memory_space=pltpu.VMEM)
    hbm = pl.BlockSpec(memory_space=pl.ANY)
    columns = keys.shape[3] // HALVES
    block = (2, 2, rows, columns)
    scale = (2, 2, 1, columns)
    bf16, f32 = jnp.bfloat16, jnp.float32
    flat = (kv_heads, 2, wide, HEAD_SIZE)
    turned = (kv_heads, 2, HEAD_SIZE, wide)
    line = (kv_heads, 2, 1, wide)
    scratch = [
        (queries.shape, bf16),
        (output.shape, bf16),
        (gradient.shape, bf16),
        (lse.shape, f32),
        (flat, bf16),
        (flat, bf16),
        (turned, bf16),
        (turned, bf16),
        (line, f32),
        (line, f32),
        ((n, HALVES) + block, bf16),
        ((n, HALVES) + block, f32),
        ((2, n - 1) + block, bf16),
        ((2, n - 1) + scale, f32),
        ((2, n - 1) + block, bf16),
        ((2, n - 1) + scale, f32),
    ]
    dqt, gk, gv = pl.pallas_call(
        functools.partial(kernel, n),
        out_shape=(
            jax.ShapeDtypeStruct(turned, f32),
            jax.ShapeDtypeStruct(keys.shape, f32),
            jax.ShapeDtypeStruct(values.shape, f32),
        ),
        in_specs=[hbm] * 6,
        out_specs=(vmem, vmem, vmem),
        scratch_shapes=[pltpu.VMEM(shape, dtype) for shape, dtype in scratch]
        + [
            pltpu.SemaphoreType.DMA((4,)),
            pltpu.SemaphoreType.DMA((HALVES, 2)),
            pltpu.SemaphoreType.DMA((2, n // 2, HALVES)),
            pltpu.SemaphoreType.DMA((2, n // 2, HALVES)),
            pltpu.SemaphoreType.DMA((2, n - 1, 2, 2)),
            pltpu.SemaphoreType.DMA((2, n - 1, 2, 2)),
        ],
        compiler_params=pltpu.CompilerParams(
            collective_id=0, has_side_effects=True, vmem_limit_bytes=64_000_000
        ),
    )(queries, keys, values, output, gradient, lse)
    return pl.pallas_call(
        finish,
        out_shape=(
            jax.ShapeDtypeStruct(queries.shape, f32),
            jax.ShapeDtypeStruct(keys.shape, f32),
            jax.ShapeDtypeStruct(values.shape, f32),
        ),
        in_specs=[vmem] * 3,
        out_specs=(vmem, vmem, vmem),
    )(dqt, gk, gv)


def solution(mesh):
    spec = P("seq", None, "dp", None)
    return jax.shard_map(
        body, mesh=mesh, in_specs=(spec,) * 6, out_specs=(spec,) * 3, check_vma=False
    )
```

time: 68.3 us -> 61.6 us (0.902)
  local copies, waits for them, and re-layouts: 5.27 us -> 0 us
  other arithmetic: 0.76 us -> 0 us
    unnamed x7 -> x0, local copies, waits for them, and re-layouts: 4.58 us -> none
    pallas_call x1, Pallas kernels: 61.4 us -> 57.1 us  [body(): pl.pallas_call(functools.partial(kernel, n), out_shape=(jax.ShapeDtypeStr...]
    pallas_call x0 -> x1, Pallas kernels: none -> 3.73 us  [body(): pl.pallas_call(finish, out_shape=(jax.ShapeDtypeStruct(queries.shape, f32...]
    mul x1 -> x0, other arithmetic: 0.76 us -> none  [body(): lse = (lse * LOG2E).reshape(kv_heads, 2, 1, wide)]
    reshape x1 -> x0, local copies, waits for them, and re-layouts: 0.69 us -> none  [body(): lse = (lse * LOG2E).reshape(kv_heads, 2, 1, wide)]
where the time goes in v2:
time: 61.6 us; the launch traced here: 61.4 us
  Pallas kernels  60.8 us (99%)
  between operations  0.64 us (1%)
    pallas_call x1, Pallas kernels, body(): pl.pallas_call(functools.partial(kernel, n), out_shape=(jax.ShapeDtypeStr...  57.1 us
    pallas_call x1, Pallas kernels, body(): pl.pallas_call(finish, out_shape=(jax.ShapeDtypeStruct(queries.shape, f32...  3.73 us

profile of v2, /device:TPU:0, one launch (start us, length us, event | category | flops | bytes accessed | tf_op | source)
XLA Modules:
  0.0 61.4 jit_solution(434765912323027341)
XLA Ops:
  0.6 57.1 %shard_map.85 = (f32[4,2,128,512]{3,2,1,0:T(8,128)}, f32[1,2,64,512]{3,2,1,0:T(8,128)}, f32[1,2,64,512]{3,2,1,0:T(8,128)}) custom-call(bf16[1,2,64,4096]{3,2,1,0:T(8,128)(2,1)} %q_hbm.1, bf16[1,2,64,512]{3,2,1,0:T(8,128)(2,1)} %k_hbm.1, bf16[1,2,64,512]{3,2,1,0:T(8,128)(2,1)} %v_hbm.1, bf16[1,2,64,4096]{3,2,1,0:T(8,128)(2,1)} %o_hbm.1, ...), custom_call_target="tpu_custom_call" | custom-call | tf_op jit(solution)/shard_map/pallas_call | solution.py:377
  57.7 3.7 %shard_map.86 = (f32[1,2,64,4096]{3,2,1,0:T(8,128)}, f32[1,2,64,512]{3,2,1,0:T(8,128)}, f32[1,2,64,512]{3,2,1,0:T(8,128)}) custom-call(f32[4,2,128,512]{3,2,1,0:T(8,128)} %get-tuple-element.6.dqt, f32[1,2,64,512]{3,2,1,0:T(8,128)} %get-tuple-element.7.gk_in, f32[1,2,64,512]{3,2,1,0:T(8,128)} %get-tuple-element.8.gv_in), custom_call_target="tpu_custom_call" | custom-call | tf_op jit(solution)/shard_map/pallas_call | solution.py:399

commit v3 on v2

--- a/solution.py
+++ b/solution.py
@@ -14,6 +14,7 @@
 MESH = pl.DeviceIdType.MESH
 KEYS, VALUES = 0, 1
 HALVES = 2
+PARTS = 4
 RIGHT, LEFT = 0, 1
 
 
@@ -56,9 +57,9 @@
     o_hbm,
     g_hbm,
     lse_hbm,
-    dqt,
-    gk_ref,
-    gv_ref,
+    gq_hbm,
+    gk_hbm,
+    gv_hbm,
     q_ref,
     o_ref,
     g_ref,
@@ -69,6 +70,10 @@
     gt,
     delta,
     lse,
+    dqt,
+    gq_ref,
+    gk_ref,
+    gv_ref,
     kv,
     part,
     coded,
@@ -77,6 +82,7 @@
     landed_scales,
     load_sem,
     own_sem,
+    out_sem,
     ag_send,
     ag_recv,
     rs_send,
@@ -170,41 +176,46 @@
 
     lax.fori_loop(0, kv_heads, prepare, 0)
 
-    def unit(keys, values, g, a, mask=None):
+    def unit(keys, values, g, a, chunk, mask=None, new=False):
         count = keys.shape[0]
-        scores = dot(keys, qt[g, a])
-        weights = jnp.exp2(scores * (scaling * LOG2E) - lse[g, a])
-        if mask is not None:
-            weights = jnp.where(mask, weights, 0.0)
-        value_part = dot(split_parts(weights), gs[g, a])
-        score_grad = weights * (dot(values, gt[g, a]) - delta[g, a])
-        split = split_parts(score_grad)
-        key_part = dot(split, qs[g, a])
         turned = jnp.transpose(keys)
-        query_part = dot(jnp.concatenate([turned, turned], axis=1), split)
-        return key_part[:count] + key_part[count:], value_part[:count] + value_part[count:], query_part
+        turned = jnp.concatenate([turned, turned], axis=1)
+        key_part = value_part = 0.0
+        for i in range(0, wide, chunk):
+            lanes = slice(i, i + chunk)
+            scores = dot(keys, qt[g, a, :, lanes])
+            weights = jnp.exp2(scores * (scaling * LOG2E) - lse[g, a, :, lanes])
+            if mask is not None:
+                weights = jnp.where(mask[:, lanes], weights, 0.0)
+            value_part += dot(split_parts(weights), gs[g, a, lanes, :])
+            score_grad = weights * (dot(values, gt[g, a, :, lanes]) - delta[g, a, :, lanes])
+            split = split_parts(score_grad)
+            key_part += dot(split, qs[g, a, lanes, :])
+            query_part = dot(turned, split)
+            if new:
+                dqt[g, a, :, lanes] = query_part
+            else:
+                dqt[g, a, :, lanes] += query_part
+        return key_part[:count] + key_part[count:], value_part[:count] + value_part[count:]
 
     def later_shard(slot, h, i):
         cols = pl.ds(i * HEAD_SIZE, HEAD_SIZE)
         g = h * some + i
         keys = kv[slot, h, KEYS, :, :, cols].reshape(2 * rows, HEAD_SIZE)
         values = kv[slot, h, VALUES, :, :, cols].reshape(2 * rows, HEAD_SIZE)
-        out = unit(keys, values, g, 1)
+        out = unit(keys, values, g, 1, wide)
         for what in (KEYS, VALUES):
             part[slot, h, what, :, :, cols] = out[what].reshape(2, rows, HEAD_SIZE)
-        dqt[g, 1] += out[2]
 
     def earlier_shard(slot, h, i):
         cols = pl.ds(i * HEAD_SIZE, HEAD_SIZE)
         g = h * some + i
         keys = kv[slot, h, KEYS, 0, :, cols]
         values = kv[slot, h, VALUES, 0, :, cols]
-        outs = [unit(keys, values, g, a) for a in range(2)]
+        outs = [unit(keys, values, g, a, wide // 2) for a in range(2)]
         for what in (KEYS, VALUES):
             part[slot, h, what, 0, :, cols] = outs[0][what] + outs[1][what]
             part[slot, h, what, 1, :, cols] = jnp.zeros((rows, HEAD_SIZE), jnp.float32)
-        for a in range(2):
-            dqt[g, a] += outs[a][2]
 
     def shard(slot, h):
         later = ring_index(lax.rem(place + slot, n), n) > me
@@ -226,13 +237,11 @@
         query_row = lax.broadcasted_iota(jnp.int32, (2 * rows, wide), 1) % rows
         keys = kv[0, h, KEYS, :, :, cols].reshape(2 * rows, HEAD_SIZE)
         values = kv[0, h, VALUES, :, :, cols].reshape(2 * rows, HEAD_SIZE)
-        first = unit(keys[:rows], values[:rows], g, 0, key_row[:rows] <= query_row[:rows])
-        second = unit(keys, values, g, 1, key_row <= query_row + rows)
+        first = unit(keys[:rows], values[:rows], g, 0, wide, key_row[:rows] <= query_row[:rows], True)
+        second = unit(keys, values, g, 1, wide, key_row <= query_row + rows, True)
         for what in (KEYS, VALUES):
             part[0, h, what, 0, :, cols] = first[what] + second[what][:rows]
             part[0, h, what, 1, :, cols] = second[what][rows:]
-        dqt[g, 0] = first[2]
-        dqt[g, 1] = second[2]
 
     def own_half(h, _):
         for i in range(some):
@@ -287,6 +296,21 @@
         gather_copy(way, way, half).wait_recv()
         shard(half, way)
         send_sums(way, half - 1, half == 1)
+
+    def write(g, _):
+        for a in range(2):
+            turned = jnp.transpose(dqt[g, a]) * scaling
+            for j in range(group):
+                head = pl.ds(pl.multiple_of((g * group + j) * HEAD_SIZE, HEAD_SIZE), HEAD_SIZE)
+                gq_ref[0, a, :, head] = turned[j * rows : (j + 1) * rows]
+        return 0
+
+    lax.fori_loop(0, kv_heads, write, 0)
+    stores = [
+        pltpu.make_async_copy(source, sink, out_sem.at[i])
+        for i, (source, sink) in enumerate(((gq_ref, gq_hbm), (gk_ref, gk_hbm), (gv_ref, gv_hbm)))
+    ]
+    stores[0].start()
 
     def far(step, _):
         for way in (RIGHT, LEFT):
@@ -306,6 +330,8 @@
                     gk_ref[0, block, :, cols] = total * scaling
                 else:
                     gv_ref[0, block, :, cols] = total
+    for copy in stores[1:]:
+        copy.start()
 
     def sent(step, _):
         for way in (RIGHT, LEFT):
@@ -325,19 +351,26 @@
     lax.fori_loop(1, half, passed, 0)
     for way in (RIGHT, LEFT):
         gather_copy(way, way, half).wait_send()
-
-
-def finish(dqt, gk_in, gv_in, gq_ref, gk_ref, gv_ref):
-    kv_heads, _, _, wide = dqt.shape
-    rows = gq_ref.shape[2]
-    for g in range(kv_heads):
-        for a in range(2):
-            turned = jnp.transpose(dqt[g, a]) * HEAD_SIZE ** (-0.5)
-            for j in range(wide // rows):
-                head = pl.ds((g * (wide // rows) + j) * HEAD_SIZE, HEAD_SIZE)
-                gq_ref[0, a, :, head] = turned[j * rows : (j + 1) * rows]
-    gk_ref[...] = gk_in[...]
-    gv_ref[...] = gv_in[...]
+    for copy in stores:
+        copy.wait()
+
+
+def finish(parts, gq_in, gk_in, gv_in, gq_hbm, gk_hbm, gv_hbm, gq_ref, gk_ref, gv_ref, in_sem, out_sem):
+    rows = gq_in.shape[2] // parts
+    pieces = [(gk_in, gk_ref, gk_hbm), (gv_in, gv_ref, gv_hbm)]
+    for a in range(2):
+        for i in range(parts):
+            at = (0, a, pl.ds(i * rows, rows))
+            pieces.append((gq_in.at[at], gq_ref.at[at], gq_hbm.at[at]))
+    loads = [pltpu.make_async_copy(x, y, in_sem.at[i]) for i, (x, y, _) in enumerate(pieces)]
+    stores = [pltpu.make_async_copy(y, z, out_sem.at[i]) for i, (_, y, z) in enumerate(pieces)]
+    for copy in loads:
+        copy.start()
+    for load, store in zip(loads, stores):
+        load.wait()
+        store.start()
+    for copy in stores:
+        copy.wait()
 
 
 def body(queries, keys, values, output, gradient, logsumexp):
@@ -347,7 +380,6 @@
     group = queries.shape[3] // keys.shape[3]
     wide = group * rows
     lse = logsumexp.transpose(0, 1, 3, 2)
-    vmem = pl.BlockSpec(memory_space=pltpu.VMEM)
     hbm = pl.BlockSpec(memory_space=pl.ANY)
     columns = keys.shape[3] // HALVES
     block = (2, 2, rows, columns)
@@ -367,6 +399,10 @@
         (turned, bf16),
         (line, f32),
         (line, f32),
+        (turned, f32),
+        (queries.shape, f32),
+        (keys.shape, f32),
+        (values.shape, f32),
         ((n, HALVES) + block, bf16),
         ((n, HALVES) + block, f32),
         ((2, n - 1) + block, bf16),
@@ -374,19 +410,20 @@
         ((2, n - 1) + block, bf16),
         ((2, n - 1) + scale, f32),
     ]
-    dqt, gk, gv = pl.pallas_call(
+    outputs = pl.pallas_call(
         functools.partial(kernel, n),
         out_shape=(
-            jax.ShapeDtypeStruct(turned, f32),
+            jax.ShapeDtypeStruct(queries.shape, f32),
             jax.ShapeDtypeStruct(keys.shape, f32),
             jax.ShapeDtypeStruct(values.shape, f32),
         ),
         in_specs=[hbm] * 6,
-        out_specs=(vmem, vmem, vmem),
+        out_specs=(hbm, hbm, hbm),
         scratch_shapes=[pltpu.VMEM(shape, dtype) for shape, dtype in scratch]
         + [
             pltpu.SemaphoreType.DMA((4,)),
             pltpu.SemaphoreType.DMA((HALVES, 2)),
+            pltpu.SemaphoreType.DMA((3,)),
             pltpu.SemaphoreType.DMA((2, n // 2, HALVES)),
             pltpu.SemaphoreType.DMA((2, n // 2, HALVES)),
             pltpu.SemaphoreType.DMA((2, n - 1, 2, 2)),
@@ -396,16 +433,16 @@
             collective_id=0, has_side_effects=True, vmem_limit_bytes=64_000_000
         ),
     )(queries, keys, values, output, gradient, lse)
+    shapes = [jax.ShapeDtypeStruct(x.shape, f32) for x in (queries, keys, values)]
     return pl.pallas_call(
-        finish,
-        out_shape=(
-            jax.ShapeDtypeStruct(queries.shape, f32),
-            jax.ShapeDtypeStruct(keys.shape, f32),
-            jax.ShapeDtypeStruct(values.shape, f32),
-        ),
-        in_specs=[vmem] * 3,
-        out_specs=(vmem, vmem, vmem),
-    )(dqt, gk, gv)
+        functools.partial(finish, PARTS),
+        out_shape=shapes,
+        in_specs=[hbm] * 3,
+        out_specs=[hbm] * 3,
+        scratch_shapes=[pltpu.VMEM(x.shape, f32) for x in shapes]
+        + [pltpu.SemaphoreType.DMA((2 + 2 * PARTS,))] * 2,
+        compiler_params=pltpu.CompilerParams(vmem_limit_bytes=64_000_000),
+    )(*outputs)
 
 
 def solution(mesh):

time: 61.6 us -> 57.4 us (0.932)
  Pallas kernels: 60.8 us -> 56.5 us
    pallas_call x1, Pallas kernels: 57.1 us -> 53.8 us  [body(): pl.pallas_call(functools.partial(kernel, n), out_shape=(jax.ShapeDtypeStr...]
    pallas_call x1, Pallas kernels: 3.73 us -> 2.6 us  [body(): pl.pallas_call(functools.partial(finish, PARTS), out_shape=shapes, in_spe...]
where the time goes in v3:
time: 57.4 us; the launch traced here: 57.3 us
  Pallas kernels  56.5 us (98%)
  between operations  0.8 us (1%)
    pallas_call x1, Pallas kernels, body(): pl.pallas_call(functools.partial(kernel, n), out_shape=(jax.ShapeDtypeStr...  53.8 us
    pallas_call x1, Pallas kernels, body(): pl.pallas_call(functools.partial(finish, PARTS), out_shape=shapes, in_spe...  2.6 us

profile of v3, /device:TPU:0, one launch (start us, length us, event | category | flops | bytes accessed | tf_op | source)
XLA Modules:
  0.0 57.3 jit_solution(4556967756167687726)
XLA Ops:
  0.6 53.8 %shard_map.85 = (f32[1,2,64,4096]{3,2,1,0:T(8,128)}, f32[1,2,64,512]{3,2,1,0:T(8,128)}, f32[1,2,64,512]{3,2,1,0:T(8,128)}) custom-call(bf16[1,2,64,4096]{3,2,1,0:T(8,128)(2,1)} %q_hbm.1, bf16[1,2,64,512]{3,2,1,0:T(8,128)(2,1)} %k_hbm.1, bf16[1,2,64,512]{3,2,1,0:T(8,128)(2,1)} %v_hbm.1, bf16[1,2,64,4096]{3,2,1,0:T(8,128)(2,1)} %o_hbm.1, ...), custom_call_target="tpu_custom_call" | custom-call | tf_op jit(solution)/shard_map/pallas_call | solution.py:413
  54.5 2.6 %shard_map.86 = (f32[1,2,64,4096]{3,2,1,0:T(8,128)}, f32[1,2,64,512]{3,2,1,0:T(8,128)}, f32[1,2,64,512]{3,2,1,0:T(8,128)}) custom-call(f32[1,2,64,4096]{3,2,1,0:T(8,128)} %get-tuple-element.6.gq_in, f32[1,2,64,512]{3,2,1,0:T(8,128)} %get-tuple-element.7.gk_in, f32[1,2,64,512]{3,2,1,0:T(8,128)} %get-tuple-element.8.gv_in), custom_call_target="tpu_custom_call" | custom-call | tf_op jit(solution)/shard_map/pallas_call | solution.py:437

commit v4 on v3

--- a/solution.py
+++ b/solution.py
@@ -88,7 +88,6 @@
     rs_send,
     rs_recv,
 ):
-    half = n // 2
     rows = k_hbm.shape[2]
     kv_heads = k_hbm.shape[3] // HEAD_SIZE
     some = kv_heads // HALVES
@@ -104,9 +103,10 @@
 
     own = [
         pltpu.make_async_copy(
-            source.at[0, :, :, pl.ds(h * columns, columns)], kv.at[0, h, what], own_sem.at[h, what]
+            source.at[0, block, :, pl.ds(h * columns, columns)], kv.at[0, h, block, what], own_sem.at[h, block, what]
         )
         for h in range(HALVES)
+        for block in range(2)
         for what, source in ((KEYS, k_hbm), (VALUES, v_hbm))
     ]
     loads = [
@@ -123,37 +123,65 @@
         pl.semaphore_signal(barrier, inc=1, device_id={"seq": neighbour}, device_id_type=MESH)
     pl.semaphore_wait(barrier, 2)
 
-    def gather_copy(way, h, distance):
+    def owner_of(slot):
+        return ring_index(lax.rem(place + slot, n), n)
+
+    def near_side(way, owner):
+        return owner % 2 == (1 if way == RIGHT else 0)
+
+    def gather_copy(way, h, distance, block):
         arrives = n - distance if way == RIGHT else distance
         held = lax.rem(n + 1 - distance, n) if way == RIGHT else distance - 1
+        which = distance - 1 if h == way else n - 2
         return pltpu.make_async_remote_copy(
-            src_ref=kv.at[held, h],
-            dst_ref=kv.at[arrives, h],
-            send_sem=ag_send.at[way, distance - 1, h],
-            recv_sem=ag_recv.at[way, distance - 1, h],
+            src_ref=kv.at[held, h, block],
+            dst_ref=kv.at[arrives, h, block],
+            send_sem=ag_send.at[way, which, block],
+            recv_sem=ag_recv.at[way, which, block],
             device_id={"seq": target[way]},
             device_id_type=MESH,
         )
 
-    def sum_copies(way, step, what):
+    def gathers(way, h, distance, sending, act):
+        hop = distance - 1 if sending else distance
+        owner = owner_of(lax.rem(n - hop, n) if way == RIGHT else hop)
+        reach = n - 2 if h == way else 1
+        act(gather_copy(way, h, distance, 0))
+
+        @pl.when(jnp.where(near_side(way, owner), distance <= owner, reach >= n - owner))
+        def _():
+            act(gather_copy(way, h, distance, 1))
+
+    def start(copy):
+        copy.start()
+
+    def wait_recv(copy):
+        copy.wait_recv()
+
+    def wait_send(copy):
+        copy.wait_send()
+
+    def sum_copies(way, step, block):
         return [
             pltpu.make_async_remote_copy(
-                src_ref=source.at[way, step, what],
-                dst_ref=sink.at[way, step, what],
-                send_sem=rs_send.at[way, step, what, i],
-                recv_sem=rs_recv.at[way, step, what, i],
+                src_ref=source.at[way, step, block],
+                dst_ref=sink.at[way, step, block],
+                send_sem=rs_send.at[way, step, block, i],
+                recv_sem=rs_recv.at[way, step, block, i],
                 device_id={"seq": target[way]},
                 device_id_type=MESH,
             )
             for i, (source, sink) in enumerate(((coded, landed), (scales, landed_scales)))
         ]
 
+    def has_late(way, step, owner):
+        return jnp.where(near_side(way, owner), owner > 0, step + 1 >= n - owner)
+
     for copy in own:
         copy.wait()
     for turn in range(HALVES):
         for way in (RIGHT, LEFT):
-            if half > 1 or turn == 0:
-                gather_copy(way, way if turn == 0 else 1 - way, 1).start()
+            gathers(way, way if turn == 0 else 1 - way, 1, True, start)
     for copy in loads:
         copy.wait()
 
@@ -201,24 +229,24 @@
     def later_shard(slot, h, i):
         cols = pl.ds(i * HEAD_SIZE, HEAD_SIZE)
         g = h * some + i
-        keys = kv[slot, h, KEYS, :, :, cols].reshape(2 * rows, HEAD_SIZE)
-        values = kv[slot, h, VALUES, :, :, cols].reshape(2 * rows, HEAD_SIZE)
+        keys = kv[slot, h, :, KEYS, :, cols].reshape(2 * rows, HEAD_SIZE)
+        values = kv[slot, h, :, VALUES, :, cols].reshape(2 * rows, HEAD_SIZE)
         out = unit(keys, values, g, 1, wide)
         for what in (KEYS, VALUES):
-            part[slot, h, what, :, :, cols] = out[what].reshape(2, rows, HEAD_SIZE)
+            part[slot, h, :, what, :, cols] = out[what].reshape(2, rows, HEAD_SIZE)
 
     def earlier_shard(slot, h, i):
         cols = pl.ds(i * HEAD_SIZE, HEAD_SIZE)
         g = h * some + i
-        keys = kv[slot, h, KEYS, 0, :, cols]
-        values = kv[slot, h, VALUES, 0, :, cols]
+        keys = kv[slot, h, 0, KEYS, :, cols]
+        values = kv[slot, h, 0, VALUES, :, cols]
         outs = [unit(keys, values, g, a, wide // 2) for a in range(2)]
         for what in (KEYS, VALUES):
-            part[slot, h, what, 0, :, cols] = outs[0][what] + outs[1][what]
-            part[slot, h, what, 1, :, cols] = jnp.zeros((rows, HEAD_SIZE), jnp.float32)
+            part[slot, h, 0, what, :, cols] = outs[0][what] + outs[1][what]
+            part[slot, h, 1, what, :, cols] = jnp.zeros((rows, HEAD_SIZE), jnp.float32)
 
     def shard(slot, h):
-        later = ring_index(lax.rem(place + slot, n), n) > me
+        later = owner_of(slot) > me
 
         @pl.when(later)
         def _():
@@ -235,13 +263,13 @@
         g = h * some + i
         key_row = lax.broadcasted_iota(jnp.int32, (2 * rows, wide), 0)
         query_row = lax.broadcasted_iota(jnp.int32, (2 * rows, wide), 1) % rows
-        keys = kv[0, h, KEYS, :, :, cols].reshape(2 * rows, HEAD_SIZE)
-        values = kv[0, h, VALUES, :, :, cols].reshape(2 * rows, HEAD_SIZE)
+        keys = kv[0, h, :, KEYS, :, cols].reshape(2 * rows, HEAD_SIZE)
+        values = kv[0, h, :, VALUES, :, cols].reshape(2 * rows, HEAD_SIZE)
         first = unit(keys[:rows], values[:rows], g, 0, wide, key_row[:rows] <= query_row[:rows], True)
         second = unit(keys, values, g, 1, wide, key_row <= query_row + rows, True)
         for what in (KEYS, VALUES):
-            part[0, h, what, 0, :, cols] = first[what] + second[what][:rows]
-            part[0, h, what, 1, :, cols] = second[what][rows:]
+            part[0, h, 0, what, :, cols] = first[what] + second[what][:rows]
+            part[0, h, 1, what, :, cols] = second[what][rows:]
 
     def own_half(h, _):
         for i in range(some):
@@ -254,48 +282,54 @@
         return n - 1 - step if way == RIGHT else 1 + step
 
     def send_sums(way, step, first):
-        for what in (KEYS, VALUES):
-            if not first:
-                for copy in sum_copies(way, step - 1, what):
+        slot = slot_of(way, step)
+        owner = owner_of(slot)
+
+        def pass_on(block, add):
+            if add:
+                for copy in sum_copies(way, step - 1, block):
                     copy.wait_recv()
-            for block in range(2):
-                total = part[slot_of(way, step), way, what, block]
-                if not first:
-                    total += decode(landed[way, step - 1, what, block], landed_scales[way, step - 1, what, block])
-                coded[way, step, what, block], scales[way, step, what, block] = encode(total)
-            for copy in sum_copies(way, step, what):
+            for what in (KEYS, VALUES):
+                total = part[slot, way, block, what]
+                if add:
+                    total += decode(landed[way, step - 1, block, what], landed_scales[way, step - 1, block, what])
+                coded[way, step, block, what], scales[way, step, block, what] = encode(total)
+            for copy in sum_copies(way, step, block):
                 copy.start()
+
+        pass_on(0, not first)
+        sends = has_late(way, step, owner)
+        if first:
+            pl.when(sends)(lambda: pass_on(1, False))
+        else:
+            adds = has_late(way, step - 1, owner)
+            pl.when(adds)(lambda: pass_on(1, True))
+            pl.when(jnp.logical_and(sends, jnp.logical_not(adds)))(lambda: pass_on(1, False))
 
     def near(step, first):
         for way in (RIGHT, LEFT):
-            gather_copy(way, way, step + 1).wait_recv()
-            gather_copy(way, way, step + 2).start()
+            gathers(way, way, step + 1, False, wait_recv)
+
+            @pl.when(step + 2 < n - 1)
+            def _():
+                gathers(way, way, step + 2, True, start)
+
         for way in (RIGHT, LEFT):
             shard(slot_of(way, step), way)
             send_sums(way, step, first)
-        for way in (RIGHT, LEFT):
-            gather_copy(way, 1 - way, step + 1).wait_recv()
-
-            @pl.when(step + 2 < half)
-            def _():
-                gather_copy(way, 1 - way, step + 2).start()
-
-        for way in (RIGHT, LEFT):
-            shard(slot_of(way, step), 1 - way)
-
-    if half > 1:
-        near(0, True)
-
-        def middle(step, _):
-            near(step, False)
-            return 0
-
-        lax.fori_loop(1, half - 1, middle, 0)
-
+
+    near(0, True)
+
+    def middle(step, _):
+        near(step, False)
+        return 0
+
+    lax.fori_loop(1, n - 2, middle, 0)
     for way in (RIGHT, LEFT):
-        gather_copy(way, way, half).wait_recv()
-        shard(half, way)
-        send_sums(way, half - 1, half == 1)
+        gathers(1 - way, way, 1, False, wait_recv)
+        shard(slot_of(way, n - 2), way)
+    for way in (RIGHT, LEFT):
+        send_sums(way, n - 2, False)
 
     def write(g, _):
         for a in range(2):
@@ -312,45 +346,52 @@
     ]
     stores[0].start()
 
-    def far(step, _):
+    def sent(step):
         for way in (RIGHT, LEFT):
-            send_sums(way, step, False)
+            for copy in sum_copies(way, step, 0):
+                copy.wait_send()
+
+            @pl.when(has_late(way, step, owner_of(slot_of(way, step))))
+            def _():
+                for copy in sum_copies(way, step, 1):
+                    copy.wait_send()
+
+    def passed(step, _):
+        sent(step)
+        for way in (RIGHT, LEFT):
+            gathers(way, way, step + 1, True, wait_send)
         return 0
 
-    lax.fori_loop(half, n - 1, far, 0)
+    lax.fori_loop(0, n - 2, passed, 0)
+    for way in (RIGHT, LEFT):
+        gathers(way, 1 - way, 1, True, wait_send)
+
     for way in (RIGHT, LEFT):
         cols = pl.ds(way * columns, columns)
-        for what in (KEYS, VALUES):
-            for copy in sum_copies(way, n - 2, what):
-                copy.wait_recv()
-            for block in range(2):
-                total = part[0, way, what, block]
-                total += decode(landed[way, n - 2, what, block], landed_scales[way, n - 2, what, block])
-                if what == KEYS:
-                    gk_ref[0, block, :, cols] = total * scaling
-                else:
-                    gv_ref[0, block, :, cols] = total
+        for block in range(2):
+
+            def finish_block(add):
+                if add:
+                    for copy in sum_copies(way, n - 2, block):
+                        copy.wait_recv()
+                for what in (KEYS, VALUES):
+                    total = part[0, way, block, what]
+                    if add:
+                        total += decode(landed[way, n - 2, block, what], landed_scales[way, n - 2, block, what])
+                    if what == KEYS:
+                        gk_ref[0, block, :, cols] = total * scaling
+                    else:
+                        gv_ref[0, block, :, cols] = total
+
+            if block == 0:
+                finish_block(True)
+            else:
+                pl.when(me > 0)(lambda: finish_block(True))
+                pl.when(me == 0)(lambda: finish_block(False))
     for copy in stores[1:]:
         copy.start()
 
-    def sent(step, _):
-        for way in (RIGHT, LEFT):
-            for what in (KEYS, VALUES):
-                for copy in sum_copies(way, step, what):
-                    copy.wait_send()
-        return 0
-
-    lax.fori_loop(0, n - 1, sent, 0)
-
-    def passed(distance, _):
-        for way in (RIGHT, LEFT):
-            for h in range(HALVES):
-                gather_copy(way, h, distance).wait_send()
-        return 0
-
-    lax.fori_loop(1, half, passed, 0)
-    for way in (RIGHT, LEFT):
-        gather_copy(way, way, half).wait_send()
+    sent(n - 2)
     for copy in stores:
         copy.wait()
 
@@ -422,10 +463,10 @@
         scratch_shapes=[pltpu.VMEM(shape, dtype) for shape, dtype in scratch]
         + [
             pltpu.SemaphoreType.DMA((4,)),
-            pltpu.SemaphoreType.DMA((HALVES, 2)),
+            pltpu.SemaphoreType.DMA((HALVES, 2, 2)),
             pltpu.SemaphoreType.DMA((3,)),
-            pltpu.SemaphoreType.DMA((2, n // 2, HALVES)),
-            pltpu.SemaphoreType.DMA((2, n // 2, HALVES)),
+            pltpu.SemaphoreType.DMA((2, n - 1, 2)),
+            pltpu.SemaphoreType.DMA((2, n - 1, 2)),
             pltpu.SemaphoreType.DMA((2, n - 1, 2, 2)),
             pltpu.SemaphoreType.DMA((2, n - 1, 2, 2)),
         ],

time: 57.4 us -> 53.6 us (0.934)
  Pallas kernels: 56.5 us -> 52.7 us
    pallas_call x1, Pallas kernels: 53.8 us -> 50.1 us  [body(): pl.pallas_call(functools.partial(kernel, n), out_shape=(jax.ShapeDtypeStr...]
where the time goes in v4:
time: 53.6 us; the launch traced here: 53.5 us
  Pallas kernels  52.7 us (98%)
  between operations  0.8 us (1%)
    pallas_call x1, Pallas kernels, body(): pl.pallas_call(functools.partial(kernel, n), out_shape=(jax.ShapeDtypeStr...  50.1 us
    pallas_call x1, Pallas kernels, body(): pl.pallas_call(functools.partial(finish, PARTS), out_shape=shapes, in_spe...  2.6 us

profile of v4, /device:TPU:0, one launch (start us, length us, event | category | flops | bytes accessed | tf_op | source)
XLA Modules:
  0.0 53.5 jit_solution(7214096797859609810)
XLA Ops:
  0.6 50.1 %shard_map.85 = (f32[1,2,64,4096]{3,2,1,0:T(8,128)}, f32[1,2,64,512]{3,2,1,0:T(8,128)}, f32[1,2,64,512]{3,2,1,0:T(8,128)}) custom-call(bf16[1,2,64,4096]{3,2,1,0:T(8,128)(2,1)} %q_hbm.1, bf16[1,2,64,512]{3,2,1,0:T(8,128)(2,1)} %k_hbm.1, bf16[1,2,64,512]{3,2,1,0:T(8,128)(2,1)} %v_hbm.1, bf16[1,2,64,4096]{3,2,1,0:T(8,128)(2,1)} %o_hbm.1, ...), custom_call_target="tpu_custom_call" | custom-call | tf_op jit(solution)/shard_map/pallas_call | solution.py:454
  50.7 2.6 %shard_map.86 = (f32[1,2,64,4096]{3,2,1,0:T(8,128)}, f32[1,2,64,512]{3,2,1,0:T(8,128)}, f32[1,2,64,512]{3,2,1,0:T(8,128)}) custom-call(f32[1,2,64,4096]{3,2,1,0:T(8,128)} %get-tuple-element.6.gq_in, f32[1,2,64,512]{3,2,1,0:T(8,128)} %get-tuple-element.7.gk_in, f32[1,2,64,512]{3,2,1,0:T(8,128)} %get-tuple-element.8.gv_in), custom_call_target="tpu_custom_call" | custom-call | tf_op jit(solution)/shard_map/pallas_call | solution.py:478

commit v5 on v4

--- a/solution.py
+++ b/solution.py
@@ -115,12 +115,11 @@
             ((q_hbm, q_ref), (g_hbm, g_ref), (o_hbm, o_ref), (lse_hbm, lse_ref))
         )
     ]
-    for copy in own + loads:
-        copy.start()
-
     barrier = pltpu.get_barrier_semaphore()
     for neighbour in (left, right):
         pl.semaphore_signal(barrier, inc=1, device_id={"seq": neighbour}, device_id_type=MESH)
+    for copy in own + loads:
+        copy.start()
     pl.semaphore_wait(barrier, 2)
 
     def owner_of(slot):
@@ -136,21 +135,21 @@
         return pltpu.make_async_remote_copy(
             src_ref=kv.at[held, h, block],
             dst_ref=kv.at[arrives, h, block],
-            send_sem=ag_send.at[way, which, block],
+            send_sem=ag_send.at[way, lax.rem(distance - 1, 2) if h == way else 2, block],
             recv_sem=ag_recv.at[way, which, block],
             device_id={"seq": target[way]},
             device_id_type=MESH,
         )
 
-    def gathers(way, h, distance, sending, act):
+    def gathers(way, h, distance, sending, act, blocks=(0, 1)):
         hop = distance - 1 if sending else distance
         owner = owner_of(lax.rem(n - hop, n) if way == RIGHT else hop)
         reach = n - 2 if h == way else 1
-        act(gather_copy(way, h, distance, 0))
-
-        @pl.when(jnp.where(near_side(way, owner), distance <= owner, reach >= n - owner))
-        def _():
-            act(gather_copy(way, h, distance, 1))
+        if 0 in blocks:
+            act(gather_copy(way, h, distance, 0))
+        if 1 in blocks:
+            needed = jnp.where(near_side(way, owner), distance <= owner, reach >= n - owner)
+            pl.when(needed)(lambda: act(gather_copy(way, h, distance, 1)))
 
     def start(copy):
         copy.start()
@@ -166,7 +165,7 @@
             pltpu.make_async_remote_copy(
                 src_ref=source.at[way, step, block],
                 dst_ref=sink.at[way, step, block],
-                send_sem=rs_send.at[way, step, block, i],
+                send_sem=rs_send.at[way, lax.rem(step, 2), block, i],
                 recv_sem=rs_recv.at[way, step, block, i],
                 device_id={"seq": target[way]},
                 device_id_type=MESH,
@@ -198,13 +197,14 @@
             delta[g, a] = jnp.sum(turned, axis=0, keepdims=True)
             qt[g, a] = jnp.transpose(qs[g, a])
             gt[g, a] = jnp.transpose(gs[g, a])
+            dqt[g, a] = jnp.zeros((HEAD_SIZE, wide), jnp.float32)
             tile = lse_ref[0, a, pl.ds(pl.multiple_of(g * group, group), group), :] * LOG2E
             lse[g, a] = jnp.concatenate([tile[j : j + 1] for j in range(group)], axis=1)
         return 0
 
     lax.fori_loop(0, kv_heads, prepare, 0)
 
-    def unit(keys, values, g, a, chunk, mask=None, new=False):
+    def unit(keys, values, g, a, chunk, mask=None):
         count = keys.shape[0]
         turned = jnp.transpose(keys)
         turned = jnp.concatenate([turned, turned], axis=1)
@@ -220,10 +220,7 @@
             split = split_parts(score_grad)
             key_part += dot(split, qs[g, a, lanes, :])
             query_part = dot(turned, split)
-            if new:
-                dqt[g, a, :, lanes] = query_part
-            else:
-                dqt[g, a, :, lanes] += query_part
+            dqt[g, a, :, lanes] += query_part
         return key_part[:count] + key_part[count:], value_part[:count] + value_part[count:]
 
     def later_shard(slot, h, i):
@@ -265,21 +262,31 @@
         query_row = lax.broadcasted_iota(jnp.int32, (2 * rows, wide), 1) % rows
         keys = kv[0, h, :, KEYS, :, cols].reshape(2 * rows, HEAD_SIZE)
         values = kv[0, h, :, VALUES, :, cols].reshape(2 * rows, HEAD_SIZE)
-        first = unit(keys[:rows], values[:rows], g, 0, wide, key_row[:rows] <= query_row[:rows], True)
-        second = unit(keys, values, g, 1, wide, key_row <= query_row + rows, True)
+        first = unit(keys[:rows], values[:rows], g, 0, wide, key_row[:rows] <= query_row[:rows])
+        second = unit(keys, values, g, 1, wide, key_row <= query_row + rows)
         for what in (KEYS, VALUES):
             part[0, h, 0, what, :, cols] = first[what] + second[what][:rows]
             part[0, h, 1, what, :, cols] = second[what][rows:]
 
-    def own_half(h, _):
-        for i in range(some):
+    def own_half(h):
+        def one(i, _):
             own_shard(h, i)
-        return 0
-
-    lax.fori_loop(0, HALVES, own_half, 0)
+            return 0
+
+        lax.fori_loop(0, some, one, 0, unroll=True)
+
+    own_half(0)
 
     def slot_of(way, step):
         return n - 1 - step if way == RIGHT else 1 + step
+
+    def sent(way, step):
+        def block_sent(block):
+            for copy in sum_copies(way, step, block):
+                copy.wait_send()
+
+        block_sent(0)
+        pl.when(has_late(way, step, owner_of(slot_of(way, step))))(lambda: block_sent(1))
 
     def send_sums(way, step, first):
         slot = slot_of(way, step)
@@ -297,6 +304,8 @@
             for copy in sum_copies(way, step, block):
                 copy.start()
 
+        if not first:
+            pl.when(step > 1)(lambda: sent(way, step - 2))
         pass_on(0, not first)
         sends = has_late(way, step, owner)
         if first:
@@ -307,18 +316,22 @@
             pl.when(jnp.logical_and(sends, jnp.logical_not(adds)))(lambda: pass_on(1, False))
 
     def near(step, first):
-        for way in (RIGHT, LEFT):
-            gathers(way, way, step + 1, False, wait_recv)
-
-            @pl.when(step + 2 < n - 1)
-            def _():
-                gathers(way, way, step + 2, True, start)
+        for block in range(2):
+            for way in (RIGHT, LEFT):
+                gathers(way, way, step + 1, False, wait_recv, (block,))
+
+                @pl.when(step + 2 < n - 1)
+                def _():
+                    if not first:
+                        gathers(way, way, step, True, wait_send, (block,))
+                    gathers(way, way, step + 2, True, start, (block,))
 
         for way in (RIGHT, LEFT):
             shard(slot_of(way, step), way)
             send_sums(way, step, first)
 
     near(0, True)
+    own_half(1)
 
     def middle(step, _):
         near(step, False)
@@ -346,25 +359,11 @@
     ]
     stores[0].start()
 
-    def sent(step):
-        for way in (RIGHT, LEFT):
-            for copy in sum_copies(way, step, 0):
-                copy.wait_send()
-
-            @pl.when(has_late(way, step, owner_of(slot_of(way, step))))
-            def _():
-                for copy in sum_copies(way, step, 1):
-                    copy.wait_send()
-
-    def passed(step, _):
-        sent(step)
-        for way in (RIGHT, LEFT):
-            gathers(way, way, step + 1, True, wait_send)
-        return 0
-
-    lax.fori_loop(0, n - 2, passed, 0)
     for way in (RIGHT, LEFT):
+        gathers(way, way, n - 3, True, wait_send)
+        gathers(way, way, n - 2, True, wait_send)
         gathers(way, 1 - way, 1, True, wait_send)
+        sent(way, n - 3)
 
     for way in (RIGHT, LEFT):
         cols = pl.ds(way * columns, columns)
@@ -391,7 +390,8 @@
     for copy in stores[1:]:
         copy.start()
 
-    sent(n - 2)
+    for way in (RIGHT, LEFT):
+        sent(way, n - 2)
     for copy in stores:
         copy.wait()
 
@@ -465,9 +465,9 @@
             pltpu.SemaphoreType.DMA((4,)),
             pltpu.SemaphoreType.DMA((HALVES, 2, 2)),
             pltpu.SemaphoreType.DMA((3,)),
+            pltpu.SemaphoreType.DMA((2, 3, 2)),
             pltpu.SemaphoreType.DMA((2, n - 1, 2)),
-            pltpu.SemaphoreType.DMA((2, n - 1, 2)),
-            pltpu.SemaphoreType.DMA((2, n - 1, 2, 2)),
+            pltpu.SemaphoreType.DMA((2, 2, 2, 2)),
             pltpu.SemaphoreType.DMA((2, n - 1, 2, 2)),
         ],
         compiler_params=pltpu.CompilerParams(

time: 53.6 us -> 53.3 us (level)
  no operation moved by 1% of the time
where the time goes in v5:
time: 53.3 us; the launch traced here: 53.1 us
  Pallas kernels  52.3 us (98%)
  between operations  0.8 us (2%)
    pallas_call x1, Pallas kernels, body(): pl.pallas_call(functools.partial(kernel, n), out_shape=(jax.ShapeDtypeStr...  49.7 us
    pallas_call x1, Pallas kernels, body(): pl.pallas_call(functools.partial(finish, PARTS), out_shape=shapes, in_spe...  2.6 us

profile of v5, /device:TPU:0, one launch (start us, length us, event | category | flops | bytes accessed | tf_op | source)
XLA Modules:
  0.0 53.1 jit_solution(2360330965059113580)
XLA Ops:
  0.6 49.7 %shard_map.85 = (f32[1,2,64,4096]{3,2,1,0:T(8,128)}, f32[1,2,64,512]{3,2,1,0:T(8,128)}, f32[1,2,64,512]{3,2,1,0:T(8,128)}) custom-call(bf16[1,2,64,4096]{3,2,1,0:T(8,128)(2,1)} %q_hbm.1, bf16[1,2,64,512]{3,2,1,0:T(8,128)(2,1)} %k_hbm.1, bf16[1,2,64,512]{3,2,1,0:T(8,128)(2,1)} %v_hbm.1, bf16[1,2,64,4096]{3,2,1,0:T(8,128)(2,1)} %o_hbm.1, ...), custom_call_target="tpu_custom_call" | custom-call | tf_op jit(solution)/shard_map/pallas_call | solution.py:454
  50.4 2.6 %shard_map.86 = (f32[1,2,64,4096]{3,2,1,0:T(8,128)}, f32[1,2,64,512]{3,2,1,0:T(8,128)}, f32[1,2,64,512]{3,2,1,0:T(8,128)}) custom-call(f32[1,2,64,4096]{3,2,1,0:T(8,128)} %get-tuple-element.6.gq_in, f32[1,2,64,512]{3,2,1,0:T(8,128)} %get-tuple-element.7.gk_in, f32[1,2,64,512]{3,2,1,0:T(8,128)} %get-tuple-element.8.gv_in), custom_call_target="tpu_custom_call" | custom-call | tf_op jit(solution)/shard_map/pallas_call | solution.py:478

commit v6 on v5

--- a/solution.py
+++ b/solution.py
@@ -101,14 +101,14 @@
     left = ring_index(lax.rem(place + n - 1, n), n)
     target = (right, left)
 
-    own = [
-        pltpu.make_async_copy(
+    own = {
+        (h, block, what): pltpu.make_async_copy(
             source.at[0, block, :, pl.ds(h * columns, columns)], kv.at[0, h, block, what], own_sem.at[h, block, what]
         )
+        for block in range(2)
         for h in range(HALVES)
-        for block in range(2)
         for what, source in ((KEYS, k_hbm), (VALUES, v_hbm))
-    ]
+    }
     loads = [
         pltpu.make_async_copy(source, sink, load_sem.at[i])
         for i, (source, sink) in enumerate(
@@ -118,7 +118,7 @@
     barrier = pltpu.get_barrier_semaphore()
     for neighbour in (left, right):
         pl.semaphore_signal(barrier, inc=1, device_id={"seq": neighbour}, device_id_type=MESH)
-    for copy in own + loads:
+    for copy in own.values():
         copy.start()
     pl.semaphore_wait(barrier, 2)
 
@@ -176,11 +176,15 @@
     def has_late(way, step, owner):
         return jnp.where(near_side(way, owner), owner > 0, step + 1 >= n - owner)
 
-    for copy in own:
-        copy.wait()
-    for turn in range(HALVES):
+    for block in range(2):
         for way in (RIGHT, LEFT):
-            gathers(way, way if turn == 0 else 1 - way, 1, True, start)
+            for what in (KEYS, VALUES):
+                own[way, block, what].wait()
+            gathers(way, way, 1, True, start, (block,))
+    for copy in loads:
+        copy.start()
+    for way in (RIGHT, LEFT):
+        gathers(way, 1 - way, 1, True, start)
     for copy in loads:
         copy.wait()
 
@@ -355,7 +359,14 @@
     lax.fori_loop(0, kv_heads, write, 0)
     stores = [
         pltpu.make_async_copy(source, sink, out_sem.at[i])
-        for i, (source, sink) in enumerate(((gq_ref, gq_hbm), (gk_ref, gk_hbm), (gv_ref, gv_hbm)))
+        for i, (source, sink) in enumerate(
+            [(gq_ref, gq_hbm)]
+            + [
+                (x.at[:, :, :, pl.ds(way * columns, columns)], y.at[:, :, :, pl.ds(way * columns, columns)])
+                for way in (RIGHT, LEFT)
+                for x, y in ((gk_ref, gk_hbm), (gv_ref, gv_hbm))
+            ]
+        )
     ]
     stores[0].start()
 
@@ -387,8 +398,8 @@
             else:
                 pl.when(me > 0)(lambda: finish_block(True))
                 pl.when(me == 0)(lambda: finish_block(False))
-    for copy in stores[1:]:
-        copy.start()
+        for copy in stores[1 + 2 * way : 3 + 2 * way]:
+            copy.start()
 
     for way in (RIGHT, LEFT):
         sent(way, n - 2)
@@ -464,7 +475,7 @@
         + [
             pltpu.SemaphoreType.DMA((4,)),
             pltpu.SemaphoreType.DMA((HALVES, 2, 2)),
-            pltpu.SemaphoreType.DMA((3,)),
+            pltpu.SemaphoreType.DMA((5,)),
             pltpu.SemaphoreType.DMA((2, 3, 2)),
             pltpu.SemaphoreType.DMA((2, n - 1, 2)),
             pltpu.SemaphoreType.DMA((2, 2, 2, 2)),

time: 53.3 us -> 52.2 us (0.979)
  Pallas kernels: 52.3 us -> 51.2 us
    pallas_call x1, Pallas kernels: 49.7 us -> 48.6 us  [body(): pl.pallas_call(functools.partial(kernel, n), out_shape=(jax.ShapeDtypeStr...]
where the time goes in v6:
time: 52.2 us; the launch traced here: 52 us
  Pallas kernels  51.2 us (98%)
  between operations  0.8 us (2%)
    pallas_call x1, Pallas kernels, body(): pl.pallas_call(functools.partial(kernel, n), out_shape=(jax.ShapeDtypeStr...  48.6 us
    pallas_call x1, Pallas kernels, body(): pl.pallas_call(functools.partial(finish, PARTS), out_shape=shapes, in_spe...  2.6 us

profile of v6, /device:TPU:0, one launch (start us, length us, event | category | flops | bytes accessed | tf_op | source)
XLA Modules:
  0.0 52.0 jit_solution(14596557505126294325)
XLA Ops:
  0.6 48.6 %shard_map.85 = (f32[1,2,64,4096]{3,2,1,0:T(8,128)}, f32[1,2,64,512]{3,2,1,0:T(8,128)}, f32[1,2,64,512]{3,2,1,0:T(8,128)}) custom-call(bf16[1,2,64,4096]{3,2,1,0:T(8,128)(2,1)} %q_hbm.1, bf16[1,2,64,512]{3,2,1,0:T(8,128)(2,1)} %k_hbm.1, bf16[1,2,64,512]{3,2,1,0:T(8,128)(2,1)} %v_hbm.1, bf16[1,2,64,4096]{3,2,1,0:T(8,128)(2,1)} %o_hbm.1, ...), custom_call_target="tpu_custom_call" | custom-call | tf_op jit(solution)/shard_map/pallas_call | solution.py:465
  49.3 2.6 %shard_map.86 = (f32[1,2,64,4096]{3,2,1,0:T(8,128)}, f32[1,2,64,512]{3,2,1,0:T(8,128)}, f32[1,2,64,512]{3,2,1,0:T(8,128)}) custom-call(f32[1,2,64,4096]{3,2,1,0:T(8,128)} %get-tuple-element.6.gq_in, f32[1,2,64,512]{3,2,1,0:T(8,128)} %get-tuple-element.7.gk_in, f32[1,2,64,512]{3,2,1,0:T(8,128)} %get-tuple-element.8.gv_in), custom_call_target="tpu_custom_call" | custom-call | tf_op jit(solution)/shard_map/pallas_call | solution.py:489

commit v7 on v6

--- a/solution.py
+++ b/solution.py
@@ -292,7 +292,7 @@
         block_sent(0)
         pl.when(has_late(way, step, owner_of(slot_of(way, step))))(lambda: block_sent(1))
 
-    def send_sums(way, step, first):
+    def send_sums(way, step, first, blocks=(0, 1)):
         slot = slot_of(way, step)
         owner = owner_of(slot)
 
@@ -308,9 +308,12 @@
             for copy in sum_copies(way, step, block):
                 copy.start()
 
-        if not first:
+        if not first and 0 in blocks:
             pl.when(step > 1)(lambda: sent(way, step - 2))
-        pass_on(0, not first)
+        if 0 in blocks:
+            pass_on(0, not first)
+        if 1 not in blocks:
+            return
         sends = has_late(way, step, owner)
         if first:
             pl.when(sends)(lambda: pass_on(1, False))
@@ -345,8 +348,9 @@
     for way in (RIGHT, LEFT):
         gathers(1 - way, way, 1, False, wait_recv)
         shard(slot_of(way, n - 2), way)
-    for way in (RIGHT, LEFT):
-        send_sums(way, n - 2, False)
+    for block in range(2):
+        for way in (RIGHT, LEFT):
+            send_sums(way, n - 2, False, (block,))
 
     def write(g, _):
         for a in range(2):

time: 52.2 us -> 52.2 us (level)
  no operation moved by 1% of the time
where the time goes in v7:
time: 52.2 us; the launch traced here: 52 us
  Pallas kernels  51.2 us (98%)
  between operations  0.8 us (2%)
    pallas_call x1, Pallas kernels, body(): pl.pallas_call(functools.partial(kernel, n), out_shape=(jax.ShapeDtypeStr...  48.6 us
    pallas_call x1, Pallas kernels, body(): pl.pallas_call(functools.partial(finish, PARTS), out_shape=shapes, in_spe...  2.6 us

profile of v7, /device:TPU:0, one launch (start us, length us, event | category | flops | bytes accessed | tf_op | source)
XLA Modules:
  0.0 52.0 jit_solution(14059658246524787590)
XLA Ops:
  0.6 48.6 %shard_map.85 = (f32[1,2,64,4096]{3,2,1,0:T(8,128)}, f32[1,2,64,512]{3,2,1,0:T(8,128)}, f32[1,2,64,512]{3,2,1,0:T(8,128)}) custom-call(bf16[1,2,64,4096]{3,2,1,0:T(8,128)(2,1)} %q_hbm.1, bf16[1,2,64,512]{3,2,1,0:T(8,128)(2,1)} %k_hbm.1, bf16[1,2,64,512]{3,2,1,0:T(8,128)(2,1)} %v_hbm.1, bf16[1,2,64,4096]{3,2,1,0:T(8,128)(2,1)} %o_hbm.1, ...), custom_call_target="tpu_custom_call" | custom-call | tf_op jit(solution)/shard_map/pallas_call | solution.py:469
  49.3 2.6 %shard_map.86 = (f32[1,2,64,4096]{3,2,1,0:T(8,128)}, f32[1,2,64,512]{3,2,1,0:T(8,128)}, f32[1,2,64,512]{3,2,1,0:T(8,128)}) custom-call(f32[1,2,64,4096]{3,2,1,0:T(8,128)} %get-tuple-element.6.gq_in, f32[1,2,64,512]{3,2,1,0:T(8,128)} %get-tuple-element.7.gk_in, f32[1,2,64,512]{3,2,1,0:T(8,128)} %get-tuple-element.8.gv_in), custom_call_target="tpu_custom_call" | custom-call | tf_op jit(solution)/shard_map/pallas_call | solution.py:493
